TPU v7x, 512 devices: a whole 4x4x16 slice. The times are simulated.
512 devices in a mesh: dom: 512 (over z, y, x, core).
Axes of the slice: x: 4, y: 4, z: 16, core: 2. Of those that a mesh axis runs over, the one named last changes fastest.
Arguments:
- tracer: float32 [40, 524288], P(None, 'dom'), may hold values from -6 to 6
- bottom_levels: int32 [524288], P('dom'), may hold values from 1 to 40
- neighbours: int32 [6, 524288], P(None, 'dom'), may hold values from 0 to 2048, as said below
- edge_weight: float32 [6, 524288], P(None, 'dom'), may hold values from 0.05 to 0.5
- ssh: float32 [524288], P('dom'), may hold values from -6 to 6
- velocity: float32 [524288], P('dom'), may hold values from -3 to 3
- send_blocks: int32 [512, 4, 2], P('dom'), may hold values from -1 to 7
- thickness: float32 [40], replicated, may hold values from 0.5 to 4
- profile: float32 [40], replicated, may hold values from -4 to 4
Outputs:
- tracer_out: float32 [40, 524288], P(None, 'dom')
- ssh_out: float32 [524288], P('dom')
- velocity_out: float32 [524288], P('dom')
Inputs may be any that keep to these rules, and one draw needn't show every extreme that they name: `neighbours`: entries 0 to 1023 are the partition's own cells, the next 1024 its received halo cells in the order of ext, and 2048 is land. `send_blocks`: -1 marks an empty slot; other entries are block numbers within the sending partition.
All inputs are finite; a program needn't handle non-finite values.
Results may differ from a plain program's by a relative error of at most 0.0003.
Values sent between devices are 32-bit elements; how exact they have to be, the bound alone decides.
A program may use at most 64 MiB of HBM per device.

v0:
```python
import jax
import jax.numpy as jnp
from jax import lax
from jax.sharding import PartitionSpec as P

BLOCK = 128
SUBSTEPS = 6


OFFSETS = (1, -1, 2, -2)
horizontal_rate = 0.5
vertical_rate = 0.5
tracer_step = 0.2
barotropic_step = 0.5
friction = 0.05


def from_behind(value, axis, by):
    peers = lax.axis_size(axis)
    pairs = [(i, i + by) for i in range(peers) if 0 <= i + by < peers]
    return lax.ppermute(value, axis, pairs)


def outgoing(field, picked_row, filled_row):
    blocks = field.reshape(field.shape[:-1] + (-1, BLOCK))
    chosen = jnp.take(blocks, picked_row, axis=-2) * filled_row[:, None]
    return chosen.reshape(field.shape[:-1] + (-1,))


def assemble(field, received):
    padding = jnp.zeros(field.shape[:-1] + (BLOCK,), field.dtype)
    return jnp.concatenate([field] + received + [padding], axis=-1)


def tracer_halo(tracer, levels, picked, filled):
    sending = [
        (
            outgoing(tracer, picked[number], filled[number]),
            outgoing(levels, picked[number], filled[number]),
        )
        for number in range(4)
    ]
    arrived = [
        from_behind((sending[number][0], sending[number][1]), "dom", OFFSETS[number])
        for number in range(4)
    ]
    ext_tracer = assemble(tracer, [arrived[number][0] for number in range(4)])
    ext_levels = assemble(levels, [arrived[number][1] for number in range(4)])
    return (ext_tracer, ext_levels)


def ssh_halo(height, picked, filled):
    sending = [outgoing(height, picked[number], filled[number]) for number in range(4)]
    arrived = [from_behind(sending[number], "dom", OFFSETS[number]) for number in range(4)]
    return assemble(height, arrived)


def shards(
    tracer, bottom_levels, neighbours, edge_weight, ssh, velocity, send_blocks, thickness, profile
):
    level_count = tracer.shape[0]
    slots = send_blocks[0]
    picked = jnp.maximum(slots, 0)
    filled = (slots >= 0).astype(jnp.float32)
    levels_f = bottom_levels.astype(jnp.float32)
    ext_tracer, ext_levels = tracer_halo(tracer, levels_f, picked, filled)
    level_index = jnp.arange(level_count).astype(jnp.float32)[:, None]
    active = (level_index < levels_f[None, :]).astype(jnp.float32)
    horizontal = jnp.zeros_like(tracer)
    for column in range(6):
        index = neighbours[column]
        near_levels = jnp.take(ext_levels, index)
        near_active = (level_index < near_levels[None, :]).astype(jnp.float32)
        near_tracer = jnp.take(ext_tracer, index, axis=1)
        horizontal = horizontal + edge_weight[column][None, :] * near_active * (
            near_tracer - tracer
        )
    horizontal = horizontal * active
    zero_level = jnp.zeros((1, tracer.shape[1]), tracer.dtype)
    below = jnp.concatenate([active[1:] * (tracer[1:] - tracer[:-1]), zero_level], axis=0)
    above = jnp.concatenate([zero_level, active[:-1] * (tracer[:-1] - tracer[1:])], axis=0)
    vertical = active * (below + above)
    tendency = horizontal_rate * horizontal + vertical_rate * vertical
    layers = active * thickness[:, None]
    forcing = jnp.sum(layers * tracer, axis=0) / jnp.sum(layers, axis=0)

    def substep(counter, carry):
        height, speed, summed = carry
        extended = ssh_halo(height, picked, filled)
        laplace = jnp.zeros_like(height)
        for column in range(6):
            laplace = laplace + edge_weight[column] * (
                jnp.take(extended, neighbours[column]) - height
            )
        speed = (1.0 - friction) * speed + barotropic_step * (laplace + forcing)
        height = height + barotropic_step * speed
        return (height, speed, summed + speed)

    height, speed, summed = lax.fori_loop(
        0, SUBSTEPS, substep, (ssh, velocity, jnp.zeros_like(velocity))
    )
    tracer_out = (
        tracer + tracer_step * tendency + active * profile[:, None] * (summed / SUBSTEPS)[None, :]
    )
    return (tracer_out, height, speed)


def solution(mesh):
    placed = (
        P(None, "dom"),
        P("dom"),
        P(None, "dom"),
        P(None, "dom"),
        P("dom"),
        P("dom"),
        P("dom", None, None),
        P(),
        P(),
    )
    return jax.shard_map(
        shards,
        mesh=mesh,
        in_specs=placed,
        out_specs=(P(None, "dom"), P("dom"), P("dom")),
        check_vma=False,
    )
```

profile of v0, /device:TPU:256, one launch (start us, length us, event | category | flops | bytes accessed | tf_op | source)
XLA Modules:
  0.0 496.0 jit_solution(14716484763080460858)
XLA Ops:
  9.0 379.1 %while.15 = (s32[]{:T(128)}, f32[1024]{0:T(1024)S(1)}, f32[1024]{0:T(1024)S(1)}, f32[1024]{0:T(1024)S(1)}, f32[6,1024]{1,0:T(8,128)S(1)}, /*index=5*/s32[4,2]{1,...) while((s32[]{:T(128)}, f32[1024]{0:T(1024)S(1)}, ...), condition=%wide.region_3.8_spmd.clone, body=%wide.region_2.0_spmd.clone.sunk | while | flops 99379 | bytes 398343 | solution.py:99
  13.8 7.5 %collective-permute-start.1 = (f32[256]{0:T(256)S(1)}, f32[256]{0:T(256)S(1)}, u32[]{:S(2)}, u32[]{:S(2)}) collective-permute-start(f32[256]{0:T(256)S(1)} %fusion.83), channel_id=1, source_target_pairs={{1,0},{2,1},{3,2},{4,3},{5,4},{6,5},{7,6},{8,7},{9,8},{10,9},{11,1... | collective-permute-start | bytes 3080 | tf_op jit(solution)/shard_map/while/body/eval_jaxpr/ppermute | solution.py:21
  24.5 9.3 %collective-permute-start.3 = (f32[256]{0:T(256)S(1)}, f32[256]{0:T(256)S(1)}, u32[]{:S(2)}, u32[]{:S(2)}) collective-permute-start(f32[256]{0:T(256)S(1)} %fusion.85), channel_id=1, source_target_pairs={{2,0},{3,1},{4,2},{5,3},{6,4},{7,5},{8,6},{9,7},{10,8},{11,9},{12,... | collective-permute-start | bytes 3080 | tf_op jit(solution)/shard_map/while/body/eval_jaxpr/ppermute | solution.py:21
  41.3 6.2 %gather_fusion.5 = f32[1024]{0:T(1024)S(1)} fusion(f32[2176]{0:T(1024)S(1)} %constant_dynamic-update-slice_fusion.29, s32[1024]{0:T(1024)S(1)} %fusion.88), kind=kCustom, calls=%fused_computation.14.clone.clone.1 | custom fusion | bytes 12288 | tf_op jit(solution)/shard_map/while/body/eval_jaxpr/jit(_take)/gather | solution.py:93
  47.5 6.2 %gather_fusion.6 = f32[1024]{0:T(1024)S(1)} fusion(f32[2176]{0:T(1024)S(1)} %constant_dynamic-update-slice_fusion.29, s32[1024]{0:T(1024)S(1)} %fusion.89), kind=kCustom, calls=%fused_computation.13.clone.clone.1 | custom fusion | bytes 12288 | tf_op jit(solution)/shard_map/while/body/eval_jaxpr/jit(_take)/gather | solution.py:93
  53.6 6.2 %gather_fusion.7 = f32[1024]{0:T(1024)S(1)} fusion(f32[2176]{0:T(1024)S(1)} %constant_dynamic-update-slice_fusion.29, s32[1024]{0:T(1024)S(1)} %fusion.90), kind=kCustom, calls=%fused_computation.12.clone.clone.1 | custom fusion | bytes 12288 | tf_op jit(solution)/shard_map/while/body/eval_jaxpr/jit(_take)/gather | solution.py:93
  59.8 6.2 %gather_fusion.8 = f32[1024]{0:T(1024)S(1)} fusion(f32[2176]{0:T(1024)S(1)} %constant_dynamic-update-slice_fusion.29, s32[1024]{0:T(1024)S(1)} %fusion.91), kind=kCustom, calls=%fused_computation.11.clone.clone.1 | custom fusion | bytes 12288 | tf_op jit(solution)/shard_map/while/body/eval_jaxpr/jit(_take)/gather | solution.py:93
  75.4 9.1 %collective-permute-start.1 = (f32[256]{0:T(256)S(1)}, f32[256]{0:T(256)S(1)}, u32[]{:S(2)}, u32[]{:S(2)}) collective-permute-start(f32[256]{0:T(256)S(1)} %fusion.83), channel_id=1, source_target_pairs={{1,0},{2,1},{3,2},{4,3},{5,4},{6,5},{7,6},{8,7},{9,8},{10,9},{11,1... | collective-permute-start | bytes 3080 | tf_op jit(solution)/shard_map/while/body/eval_jaxpr/ppermute | solution.py:21
  87.7 9.3 %collective-permute-start.3 = (f32[256]{0:T(256)S(1)}, f32[256]{0:T(256)S(1)}, u32[]{:S(2)}, u32[]{:S(2)}) collective-permute-start(f32[256]{0:T(256)S(1)} %fusion.85), channel_id=1, source_target_pairs={{2,0},{3,1},{4,2},{5,3},{6,4},{7,5},{8,6},{9,7},{10,8},{11,9},{12,... | collective-permute-start | bytes 3080 | tf_op jit(solution)/shard_map/while/body/eval_jaxpr/ppermute | solution.py:21
  104.5 6.2 %gather_fusion.5 = f32[1024]{0:T(1024)S(1)} fusion(f32[2176]{0:T(1024)S(1)} %constant_dynamic-update-slice_fusion.29, s32[1024]{0:T(1024)S(1)} %fusion.88), kind=kCustom, calls=%fused_computation.14.clone.clone.1 | custom fusion | bytes 12288 | tf_op jit(solution)/shard_map/while/body/eval_jaxpr/jit(_take)/gather | solution.py:93
  110.6 6.2 %gather_fusion.6 = f32[1024]{0:T(1024)S(1)} fusion(f32[2176]{0:T(1024)S(1)} %constant_dynamic-update-slice_fusion.29, s32[1024]{0:T(1024)S(1)} %fusion.89), kind=kCustom, calls=%fused_computation.13.clone.clone.1 | custom fusion | bytes 12288 | tf_op jit(solution)/shard_map/while/body/eval_jaxpr/jit(_take)/gather | solution.py:93
  116.8 6.2 %gather_fusion.7 = f32[1024]{0:T(1024)S(1)} fusion(f32[2176]{0:T(1024)S(1)} %constant_dynamic-update-slice_fusion.29, s32[1024]{0:T(1024)S(1)} %fusion.90), kind=kCustom, calls=%fused_computation.12.clone.clone.1 | custom fusion | bytes 12288 | tf_op jit(solution)/shard_map/while/body/eval_jaxpr/jit(_take)/gather | solution.py:93
  123.0 6.2 %gather_fusion.8 = f32[1024]{0:T(1024)S(1)} fusion(f32[2176]{0:T(1024)S(1)} %constant_dynamic-update-slice_fusion.29, s32[1024]{0:T(1024)S(1)} %fusion.91), kind=kCustom, calls=%fused_computation.11.clone.clone.1 | custom fusion | bytes 12288 | tf_op jit(solution)/shard_map/while/body/eval_jaxpr/jit(_take)/gather | solution.py:93
  129.1 6.2 %gather_fusion.9 = f32[1024]{0:T(1024)S(1)} fusion(f32[2176]{0:T(1024)S(1)} %constant_dynamic-update-slice_fusion.29, s32[1024]{0:T(1024)S(1)} %fusion.92), kind=kCustom, calls=%fused_computation.1.clone.clone.1 | custom fusion | bytes 12288 | tf_op jit(solution)/shard_map/while/body/eval_jaxpr/jit(_take)/gather | solution.py:93
  138.6 9.1 %collective-permute-start.1 = (f32[256]{0:T(256)S(1)}, f32[256]{0:T(256)S(1)}, u32[]{:S(2)}, u32[]{:S(2)}) collective-permute-start(f32[256]{0:T(256)S(1)} %fusion.83), channel_id=1, source_target_pairs={{1,0},{2,1},{3,2},{4,3},{5,4},{6,5},{7,6},{8,7},{9,8},{10,9},{11,1... | collective-permute-start | bytes 3080 | tf_op jit(solution)/shard_map/while/body/eval_jaxpr/ppermute | solution.py:21
  150.9 9.3 %collective-permute-start.3 = (f32[256]{0:T(256)S(1)}, f32[256]{0:T(256)S(1)}, u32[]{:S(2)}, u32[]{:S(2)}) collective-permute-start(f32[256]{0:T(256)S(1)} %fusion.85), channel_id=1, source_target_pairs={{2,0},{3,1},{4,2},{5,3},{6,4},{7,5},{8,6},{9,7},{10,8},{11,9},{12,... | collective-permute-start | bytes 3080 | tf_op jit(solution)/shard_map/while/body/eval_jaxpr/ppermute | solution.py:21
  167.6 6.2 %gather_fusion.5 = f32[1024]{0:T(1024)S(1)} fusion(f32[2176]{0:T(1024)S(1)} %constant_dynamic-update-slice_fusion.29, s32[1024]{0:T(1024)S(1)} %fusion.88), kind=kCustom, calls=%fused_computation.14.clone.clone.1 | custom fusion | bytes 12288 | tf_op jit(solution)/shard_map/while/body/eval_jaxpr/jit(_take)/gather | solution.py:93
  180.0 6.2 %gather_fusion.7 = f32[1024]{0:T(1024)S(1)} fusion(f32[2176]{0:T(1024)S(1)} %constant_dynamic-update-slice_fusion.29, s32[1024]{0:T(1024)S(1)} %fusion.90), kind=kCustom, calls=%fused_computation.12.clone.clone.1 | custom fusion | bytes 12288 | tf_op jit(solution)/shard_map/while/body/eval_jaxpr/jit(_take)/gather | solution.py:93
  186.1 6.2 %gather_fusion.8 = f32[1024]{0:T(1024)S(1)} fusion(f32[2176]{0:T(1024)S(1)} %constant_dynamic-update-slice_fusion.29, s32[1024]{0:T(1024)S(1)} %fusion.91), kind=kCustom, calls=%fused_computation.11.clone.clone.1 | custom fusion | bytes 12288 | tf_op jit(solution)/shard_map/while/body/eval_jaxpr/jit(_take)/gather | solution.py:93
  192.3 6.2 %gather_fusion.9 = f32[1024]{0:T(1024)S(1)} fusion(f32[2176]{0:T(1024)S(1)} %constant_dynamic-update-slice_fusion.29, s32[1024]{0:T(1024)S(1)} %fusion.92), kind=kCustom, calls=%fused_computation.1.clone.clone.1 | custom fusion | bytes 12288 | tf_op jit(solution)/shard_map/while/body/eval_jaxpr/jit(_take)/gather | solution.py:93
  201.8 9.1 %collective-permute-start.1 = (f32[256]{0:T(256)S(1)}, f32[256]{0:T(256)S(1)}, u32[]{:S(2)}, u32[]{:S(2)}) collective-permute-start(f32[256]{0:T(256)S(1)} %fusion.83), channel_id=1, source_target_pairs={{1,0},{2,1},{3,2},{4,3},{5,4},{6,5},{7,6},{8,7},{9,8},{10,9},{11,1... | collective-permute-start | bytes 3080 | tf_op jit(solution)/shard_map/while/body/eval_jaxpr/ppermute | solution.py:21
  214.0 9.3 %collective-permute-start.3 = (f32[256]{0:T(256)S(1)}, f32[256]{0:T(256)S(1)}, u32[]{:S(2)}, u32[]{:S(2)}) collective-permute-start(f32[256]{0:T(256)S(1)} %fusion.85), channel_id=1, source_target_pairs={{2,0},{3,1},{4,2},{5,3},{6,4},{7,5},{8,6},{9,7},{10,8},{11,9},{12,... | collective-permute-start | bytes 3080 | tf_op jit(solution)/shard_map/while/body/eval_jaxpr/ppermute | solution.py:21
  230.8 6.2 %gather_fusion.5 = f32[1024]{0:T(1024)S(1)} fusion(f32[2176]{0:T(1024)S(1)} %constant_dynamic-update-slice_fusion.29, s32[1024]{0:T(1024)S(1)} %fusion.88), kind=kCustom, calls=%fused_computation.14.clone.clone.1 | custom fusion | bytes 12288 | tf_op jit(solution)/shard_map/while/body/eval_jaxpr/jit(_take)/gather | solution.py:93
  237.0 6.2 %gather_fusion.6 = f32[1024]{0:T(1024)S(1)} fusion(f32[2176]{0:T(1024)S(1)} %constant_dynamic-update-slice_fusion.29, s32[1024]{0:T(1024)S(1)} %fusion.89), kind=kCustom, calls=%fused_computation.13.clone.clone.1 | custom fusion | bytes 12288 | tf_op jit(solution)/shard_map/while/body/eval_jaxpr/jit(_take)/gather | solution.py:93
  249.3 6.2 %gather_fusion.8 = f32[1024]{0:T(1024)S(1)} fusion(f32[2176]{0:T(1024)S(1)} %constant_dynamic-update-slice_fusion.29, s32[1024]{0:T(1024)S(1)} %fusion.91), kind=kCustom, calls=%fused_computation.11.clone.clone.1 | custom fusion | bytes 12288 | tf_op jit(solution)/shard_map/while/body/eval_jaxpr/jit(_take)/gather | solution.py:93
  255.5 6.2 %gather_fusion.9 = f32[1024]{0:T(1024)S(1)} fusion(f32[2176]{0:T(1024)S(1)} %constant_dynamic-update-slice_fusion.29, s32[1024]{0:T(1024)S(1)} %fusion.92), kind=kCustom, calls=%fused_computation.1.clone.clone.1 | custom fusion | bytes 12288 | tf_op jit(solution)/shard_map/while/body/eval_jaxpr/jit(_take)/gather | solution.py:93
  264.9 9.1 %collective-permute-start.1 = (f32[256]{0:T(256)S(1)}, f32[256]{0:T(256)S(1)}, u32[]{:S(2)}, u32[]{:S(2)}) collective-permute-start(f32[256]{0:T(256)S(1)} %fusion.83), channel_id=1, source_target_pairs={{1,0},{2,1},{3,2},{4,3},{5,4},{6,5},{7,6},{8,7},{9,8},{10,9},{11,1... | collective-permute-start | bytes 3080 | tf_op jit(solution)/shard_map/while/body/eval_jaxpr/ppermute | solution.py:21
  277.2 9.3 %collective-permute-start.3 = (f32[256]{0:T(256)S(1)}, f32[256]{0:T(256)S(1)}, u32[]{:S(2)}, u32[]{:S(2)}) collective-permute-start(f32[256]{0:T(256)S(1)} %fusion.85), channel_id=1, source_target_pairs={{2,0},{3,1},{4,2},{5,3},{6,4},{7,5},{8,6},{9,7},{10,8},{11,9},{12,... | collective-permute-start | bytes 3080 | tf_op jit(solution)/shard_map/while/body/eval_jaxpr/ppermute | solution.py:21
  294.0 6.2 %gather_fusion.5 = f32[1024]{0:T(1024)S(1)} fusion(f32[2176]{0:T(1024)S(1)} %constant_dynamic-update-slice_fusion.29, s32[1024]{0:T(1024)S(1)} %fusion.88), kind=kCustom, calls=%fused_computation.14.clone.clone.1 | custom fusion | bytes 12288 | tf_op jit(solution)/shard_map/while/body/eval_jaxpr/jit(_take)/gather | solution.py:93
  300.2 6.2 %gather_fusion.6 = f32[1024]{0:T(1024)S(1)} fusion(f32[2176]{0:T(1024)S(1)} %constant_dynamic-update-slice_fusion.29, s32[1024]{0:T(1024)S(1)} %fusion.89), kind=kCustom, calls=%fused_computation.13.clone.clone.1 | custom fusion | bytes 12288 | tf_op jit(solution)/shard_map/while/body/eval_jaxpr/jit(_take)/gather | solution.py:93
  306.3 6.2 %gather_fusion.7 = f32[1024]{0:T(1024)S(1)} fusion(f32[2176]{0:T(1024)S(1)} %constant_dynamic-update-slice_fusion.29, s32[1024]{0:T(1024)S(1)} %fusion.90), kind=kCustom, calls=%fused_computation.12.clone.clone.1 | custom fusion | bytes 12288 | tf_op jit(solution)/shard_map/while/body/eval_jaxpr/jit(_take)/gather | solution.py:93
  312.5 6.2 %gather_fusion.8 = f32[1024]{0:T(1024)S(1)} fusion(f32[2176]{0:T(1024)S(1)} %constant_dynamic-update-slice_fusion.29, s32[1024]{0:T(1024)S(1)} %fusion.91), kind=kCustom, calls=%fused_computation.11.clone.clone.1 | custom fusion | bytes 12288 | tf_op jit(solution)/shard_map/while/body/eval_jaxpr/jit(_take)/gather | solution.py:93
  318.6 6.2 %gather_fusion.9 = f32[1024]{0:T(1024)S(1)} fusion(f32[2176]{0:T(1024)S(1)} %constant_dynamic-update-slice_fusion.29, s32[1024]{0:T(1024)S(1)} %fusion.92), kind=kCustom, calls=%fused_computation.1.clone.clone.1 | custom fusion | bytes 12288 | tf_op jit(solution)/shard_map/while/body/eval_jaxpr/jit(_take)/gather | solution.py:93
  328.1 9.1 %collective-permute-start.1 = (f32[256]{0:T(256)S(1)}, f32[256]{0:T(256)S(1)}, u32[]{:S(2)}, u32[]{:S(2)}) collective-permute-start(f32[256]{0:T(256)S(1)} %fusion.83), channel_id=1, source_target_pairs={{1,0},{2,1},{3,2},{4,3},{5,4},{6,5},{7,6},{8,7},{9,8},{10,9},{11,1... | collective-permute-start | bytes 3080 | tf_op jit(solution)/shard_map/while/body/eval_jaxpr/ppermute | solution.py:21
  340.4 9.3 %collective-permute-start.3 = (f32[256]{0:T(256)S(1)}, f32[256]{0:T(256)S(1)}, u32[]{:S(2)}, u32[]{:S(2)}) collective-permute-start(f32[256]{0:T(256)S(1)} %fusion.85), channel_id=1, source_target_pairs={{2,0},{3,1},{4,2},{5,3},{6,4},{7,5},{8,6},{9,7},{10,8},{11,9},{12,... | collective-permute-start | bytes 3080 | tf_op jit(solution)/shard_map/while/body/eval_jaxpr/ppermute | solution.py:21
  357.2 6.2 %gather_fusion.5 = f32[1024]{0:T(1024)S(1)} fusion(f32[2176]{0:T(1024)S(1)} %constant_dynamic-update-slice_fusion.29, s32[1024]{0:T(1024)S(1)} %fusion.88), kind=kCustom, calls=%fused_computation.14.clone.clone.1 | custom fusion | bytes 12288 | tf_op jit(solution)/shard_map/while/body/eval_jaxpr/jit(_take)/gather | solution.py:93
  363.3 6.2 %gather_fusion.6 = f32[1024]{0:T(1024)S(1)} fusion(f32[2176]{0:T(1024)S(1)} %constant_dynamic-update-slice_fusion.29, s32[1024]{0:T(1024)S(1)} %fusion.89), kind=kCustom, calls=%fused_computation.13.clone.clone.1 | custom fusion | bytes 12288 | tf_op jit(solution)/shard_map/while/body/eval_jaxpr/jit(_take)/gather | solution.py:93
  369.5 6.2 %gather_fusion.7 = f32[1024]{0:T(1024)S(1)} fusion(f32[2176]{0:T(1024)S(1)} %constant_dynamic-update-slice_fusion.29, s32[1024]{0:T(1024)S(1)} %fusion.90), kind=kCustom, calls=%fused_computation.12.clone.clone.1 | custom fusion | bytes 12288 | tf_op jit(solution)/shard_map/while/body/eval_jaxpr/jit(_take)/gather | solution.py:93
  375.7 6.2 %gather_fusion.8 = f32[1024]{0:T(1024)S(1)} fusion(f32[2176]{0:T(1024)S(1)} %constant_dynamic-update-slice_fusion.29, s32[1024]{0:T(1024)S(1)} %fusion.91), kind=kCustom, calls=%fused_computation.11.clone.clone.1 | custom fusion | bytes 12288 | tf_op jit(solution)/shard_map/while/body/eval_jaxpr/jit(_take)/gather | solution.py:93
  381.8 6.2 %gather_fusion.9 = f32[1024]{0:T(1024)S(1)} fusion(f32[2176]{0:T(1024)S(1)} %constant_dynamic-update-slice_fusion.29, s32[1024]{0:T(1024)S(1)} %fusion.92), kind=kCustom, calls=%fused_computation.1.clone.clone.1 | custom fusion | bytes 12288 | tf_op jit(solution)/shard_map/while/body/eval_jaxpr/jit(_take)/gather | solution.py:93
  393.2 9.6 %collective-permute-start.7 = (f32[256]{0:T(256)S(1)}, f32[256]{0:T(256)S(1)}, u32[]{:S(2)}, u32[]{:S(2)}) collective-permute-start(f32[256]{0:T(256)S(1)} %fusion.53), channel_id=1, source_target_pairs={{2,0},{3,1},{4,2},{5,3},{6,4},{7,5},{8,6},{9,7},{10,8},{11,9},{12,... | collective-permute-start | bytes 3080 | tf_op jit(solution)/shard_map/ppermute | solution.py:21
  408.3 8.9 %collective-permute-start.9 = (f32[40,256]{1,0:T(8,128)S(1)}, f32[40,256]{1,0:T(8,128)S(1)}, u32[]{:S(2)}, u32[]{:S(2)}) collective-permute-start(f32[40,256]{1,0:T(8,128)S(1)} %copy_bitcast_fusion.3), channel_id=1, source_target_pairs={{1,0},{2,1},{3,2},{4,3},{5,4},{6,5},{7,6},{8,7},{9,8},{10,9},{11,1... | collective-permute-start | bytes 122888 | tf_op jit(solution)/shard_map/ppermute | solution.py:21
  419.1 9.4 %collective-permute-start.11 = (f32[40,256]{1,0:T(8,128)S(1)}, f32[40,256]{1,0:T(8,128)S(1)}, u32[]{:S(2)}, u32[]{:S(2)}) collective-permute-start(f32[40,256]{1,0:T(8,128)S(1)} %copy_bitcast_fusion.1), channel_id=1, source_target_pairs={{2,0},{3,1},{4,2},{5,3},{6,4},{7,5},{8,6},{9,7},{10,8},{11,9},{12,... | collective-permute-start | bytes 122888 | tf_op jit(solution)/shard_map/ppermute | solution.py:21
  428.6 6.2 %gather_fusion.14 = f32[1024]{0:T(1024)S(1)} fusion(f32[2176]{0:T(1024)S(1)} %constant_dynamic-update-slice_fusion.13, s32[1024]{0:T(1024)S(1)} %get-tuple-element.233), kind=kCustom, calls=%fused_computation.16.clone | custom fusion | bytes 12288 | tf_op jit(solution)/shard_map/jit(_take)/gather | solution.py:72
  434.7 6.2 %gather_fusion.20 = f32[1024]{0:T(1024)S(1)} fusion(f32[2176]{0:T(1024)S(1)} %constant_dynamic-update-slice_fusion.13, s32[1024]{0:T(1024)S(1)} %get-tuple-element.234), kind=kCustom, calls=%fused_computation.17.clone | custom fusion | bytes 12288 | tf_op jit(solution)/shard_map/jit(_take)/gather | solution.py:72
  440.9 6.2 %gather_fusion.22 = f32[1024]{0:T(1024)S(1)} fusion(f32[2176]{0:T(1024)S(1)} %constant_dynamic-update-slice_fusion.13, s32[1024]{0:T(1024)S(1)} %get-tuple-element.235), kind=kCustom, calls=%fused_computation.18.clone | custom fusion | bytes 12288 | tf_op jit(solution)/shard_map/jit(_take)/gather | solution.py:72
  447.1 6.2 %gather_fusion.24 = f32[1024]{0:T(1024)S(1)} fusion(f32[2176]{0:T(1024)S(1)} %constant_dynamic-update-slice_fusion.13, s32[1024]{0:T(1024)S(1)} %get-tuple-element.236), kind=kCustom, calls=%fused_computation.19.clone | custom fusion | bytes 12288 | tf_op jit(solution)/shard_map/jit(_take)/gather | solution.py:72
  488.9 6.2 %fusion.30 = f32[40,1024]{0,1:T(8,128)S(1)} fusion(f32[40,1024]{0,1:T(8,128)S(1)} %copy.88, f32[1024,40]{1,0:T(8,128)} %gather_fusion.29, f32[1024,40]{1,0:T(8,128)} %gather_fusion.27, f32[1024,40]{1,0:T(8,128)} %gather_fusion.25, f32[1024,40]{1,0:T(8,128)} %gather_fusion.23, f32[1024,40]{1,0:T(8,128)} %gather_fusion.21, f32[1024,40]{1,0:T(8,128)S(1)} %gather_fusion.19, ...), kind=kLoop, calls=%fused_computation.105 | loop fusion | flops 1843200 | bytes 1694016 | tf_op jit(solution)/shard_map/add | solution.py:103
  (331 shorter events, 159.4 us)
Async XLA Ops:
  0.6 8.3 %copy-start.3 = (s32[6,1024]{1,0:T(8,128)S(1)}, s32[6,1024]{1,0:T(8,128)}, u32[]{:S(2)}) copy-start(s32[6,1024]{1,0:T(8,128)} %param.21) | copy-start | bytes 73732
  0.6 8.3 %copy-start.4 = (f32[6,1024]{1,0:T(8,128)S(1)}, f32[6,1024]{1,0:T(8,128)}, u32[]{:S(2)}) copy-start(f32[6,1024]{1,0:T(8,128)} %param.22) | copy-start | bytes 73732
  0.7 8.3 %copy-start.1 = (f32[1024]{0:T(1024)S(1)}, f32[1024]{0:T(1024)}, u32[]{:S(2)}) copy-start(f32[1024]{0:T(1024)} %param.23) | copy-start | bytes 12292
  0.7 8.3 %copy-start.6 = (f32[1024]{0:T(1024)S(1)}, f32[1024]{0:T(1024)}, u32[]{:S(2)}) copy-start(f32[1024]{0:T(1024)} %param.24) | copy-start | bytes 12292
  3.9 404.4 %collective-permute-start.4 = (f32[256]{0:T(256)S(1)}, f32[256]{0:T(256)S(1)}, u32[]{:S(2)}, u32[]{:S(2)}) collective-permute-start(f32[256]{0:T(256)S(1)} %fusion.56), channel_id=1, source_target_pairs={{0,1},{1,2},{2,3},{3,4},{4,5},{5,6},{6,7},{7,8},{8,9},{9,10},{10,1... | collective-permute-start | bytes 3080 | tf_op jit(solution)/shard_map/ppermute | solution.py:21
  8.9 393.9 %copy-start.7 = (s32[1024]{0:T(1024)S(1)}, s32[1024]{0:T(1024)}, u32[]{:S(2)}) copy-start(s32[1024]{0:T(1024)} %param.20) | copy-start | bytes 12292
  9.0 393.9 %copy-start.2 = (f32[40,1024]{1,0:T(8,128)S(1)}, f32[40,1024]{1,0:T(8,128)}, u32[]{:S(2)}) copy-start(f32[40,1024]{1,0:T(8,128)} %param.19) | copy-start | bytes 491524
  9.7 24.4 %collective-permute-start = (f32[256]{0:T(256)S(1)}, f32[256]{0:T(256)S(1)}, u32[]{:S(2)}, u32[]{:S(2)}) collective-permute-start(f32[256]{0:T(256)S(1)} %fusion.82), channel_id=1, source_target_pairs={{0,1},{1,2},{2,3},{3,4},{4,5},{5,6},{6,7},{7,8},{8,9},{9,10},{10,1... | collective-permute-start | bytes 3080 | tf_op jit(solution)/shard_map/while/body/eval_jaxpr/ppermute | solution.py:21
  13.8 20.2 %collective-permute-start.1 = (f32[256]{0:T(256)S(1)}, f32[256]{0:T(256)S(1)}, u32[]{:S(2)}, u32[]{:S(2)}) collective-permute-start(f32[256]{0:T(256)S(1)} %fusion.83), channel_id=1, source_target_pairs={{1,0},{2,1},{3,2},{4,3},{5,4},{6,5},{7,6},{8,7},{9,8},{10,9},{11,1... | collective-permute-start | bytes 3080 | tf_op jit(solution)/shard_map/while/body/eval_jaxpr/ppermute | solution.py:21
  21.9 12.1 %collective-permute-start.2 = (f32[256]{0:T(256)S(1)}, f32[256]{0:T(256)S(1)}, u32[]{:S(2)}, u32[]{:S(2)}) collective-permute-start(f32[256]{0:T(256)S(1)} %fusion.84), channel_id=1, source_target_pairs={{0,2},{1,3},{2,4},{3,5},{4,6},{5,7},{6,8},{7,9},{8,10},{9,11},{10,... | collective-permute-start | bytes 3080 | tf_op jit(solution)/shard_map/while/body/eval_jaxpr/ppermute | solution.py:21
  24.5 10.6 %collective-permute-start.3 = (f32[256]{0:T(256)S(1)}, f32[256]{0:T(256)S(1)}, u32[]{:S(2)}, u32[]{:S(2)}) collective-permute-start(f32[256]{0:T(256)S(1)} %fusion.85), channel_id=1, source_target_pairs={{2,0},{3,1},{4,2},{5,3},{6,4},{7,5},{8,6},{9,7},{10,8},{11,9},{12,... | collective-permute-start | bytes 3080 | tf_op jit(solution)/shard_map/while/body/eval_jaxpr/ppermute | solution.py:21
  72.8 24.4 %collective-permute-start = (f32[256]{0:T(256)S(1)}, f32[256]{0:T(256)S(1)}, u32[]{:S(2)}, u32[]{:S(2)}) collective-permute-start(f32[256]{0:T(256)S(1)} %fusion.82), channel_id=1, source_target_pairs={{0,1},{1,2},{2,3},{3,4},{4,5},{5,6},{6,7},{7,8},{8,9},{9,10},{10,1... | collective-permute-start | bytes 3080 | tf_op jit(solution)/shard_map/while/body/eval_jaxpr/ppermute | solution.py:21
  75.4 21.8 %collective-permute-start.1 = (f32[256]{0:T(256)S(1)}, f32[256]{0:T(256)S(1)}, u32[]{:S(2)}, u32[]{:S(2)}) collective-permute-start(f32[256]{0:T(256)S(1)} %fusion.83), channel_id=1, source_target_pairs={{1,0},{2,1},{3,2},{4,3},{5,4},{6,5},{7,6},{8,7},{9,8},{10,9},{11,1... | collective-permute-start | bytes 3080 | tf_op jit(solution)/shard_map/while/body/eval_jaxpr/ppermute | solution.py:21
  85.1 12.1 %collective-permute-start.2 = (f32[256]{0:T(256)S(1)}, f32[256]{0:T(256)S(1)}, u32[]{:S(2)}, u32[]{:S(2)}) collective-permute-start(f32[256]{0:T(256)S(1)} %fusion.84), channel_id=1, source_target_pairs={{0,2},{1,3},{2,4},{3,5},{4,6},{5,7},{6,8},{7,9},{8,10},{9,11},{10,... | collective-permute-start | bytes 3080 | tf_op jit(solution)/shard_map/while/body/eval_jaxpr/ppermute | solution.py:21
  87.7 10.6 %collective-permute-start.3 = (f32[256]{0:T(256)S(1)}, f32[256]{0:T(256)S(1)}, u32[]{:S(2)}, u32[]{:S(2)}) collective-permute-start(f32[256]{0:T(256)S(1)} %fusion.85), channel_id=1, source_target_pairs={{2,0},{3,1},{4,2},{5,3},{6,4},{7,5},{8,6},{9,7},{10,8},{11,9},{12,... | collective-permute-start | bytes 3080 | tf_op jit(solution)/shard_map/while/body/eval_jaxpr/ppermute | solution.py:21
  136.0 24.4 %collective-permute-start = (f32[256]{0:T(256)S(1)}, f32[256]{0:T(256)S(1)}, u32[]{:S(2)}, u32[]{:S(2)}) collective-permute-start(f32[256]{0:T(256)S(1)} %fusion.82), channel_id=1, source_target_pairs={{0,1},{1,2},{2,3},{3,4},{4,5},{5,6},{6,7},{7,8},{8,9},{9,10},{10,1... | collective-permute-start | bytes 3080 | tf_op jit(solution)/shard_map/while/body/eval_jaxpr/ppermute | solution.py:21
  138.6 21.8 %collective-permute-start.1 = (f32[256]{0:T(256)S(1)}, f32[256]{0:T(256)S(1)}, u32[]{:S(2)}, u32[]{:S(2)}) collective-permute-start(f32[256]{0:T(256)S(1)} %fusion.83), channel_id=1, source_target_pairs={{1,0},{2,1},{3,2},{4,3},{5,4},{6,5},{7,6},{8,7},{9,8},{10,9},{11,1... | collective-permute-start | bytes 3080 | tf_op jit(solution)/shard_map/while/body/eval_jaxpr/ppermute | solution.py:21
  148.3 12.1 %collective-permute-start.2 = (f32[256]{0:T(256)S(1)}, f32[256]{0:T(256)S(1)}, u32[]{:S(2)}, u32[]{:S(2)}) collective-permute-start(f32[256]{0:T(256)S(1)} %fusion.84), channel_id=1, source_target_pairs={{0,2},{1,3},{2,4},{3,5},{4,6},{5,7},{6,8},{7,9},{8,10},{9,11},{10,... | collective-permute-start | bytes 3080 | tf_op jit(solution)/shard_map/while/body/eval_jaxpr/ppermute | solution.py:21
  150.9 10.6 %collective-permute-start.3 = (f32[256]{0:T(256)S(1)}, f32[256]{0:T(256)S(1)}, u32[]{:S(2)}, u32[]{:S(2)}) collective-permute-start(f32[256]{0:T(256)S(1)} %fusion.85), channel_id=1, source_target_pairs={{2,0},{3,1},{4,2},{5,3},{6,4},{7,5},{8,6},{9,7},{10,8},{11,9},{12,... | collective-permute-start | bytes 3080 | tf_op jit(solution)/shard_map/while/body/eval_jaxpr/ppermute | solution.py:21
  199.2 24.4 %collective-permute-start = (f32[256]{0:T(256)S(1)}, f32[256]{0:T(256)S(1)}, u32[]{:S(2)}, u32[]{:S(2)}) collective-permute-start(f32[256]{0:T(256)S(1)} %fusion.82), channel_id=1, source_target_pairs={{0,1},{1,2},{2,3},{3,4},{4,5},{5,6},{6,7},{7,8},{8,9},{9,10},{10,1... | collective-permute-start | bytes 3080 | tf_op jit(solution)/shard_map/while/body/eval_jaxpr/ppermute | solution.py:21
  201.8 21.8 %collective-permute-start.1 = (f32[256]{0:T(256)S(1)}, f32[256]{0:T(256)S(1)}, u32[]{:S(2)}, u32[]{:S(2)}) collective-permute-start(f32[256]{0:T(256)S(1)} %fusion.83), channel_id=1, source_target_pairs={{1,0},{2,1},{3,2},{4,3},{5,4},{6,5},{7,6},{8,7},{9,8},{10,9},{11,1... | collective-permute-start | bytes 3080 | tf_op jit(solution)/shard_map/while/body/eval_jaxpr/ppermute | solution.py:21
  211.5 12.1 %collective-permute-start.2 = (f32[256]{0:T(256)S(1)}, f32[256]{0:T(256)S(1)}, u32[]{:S(2)}, u32[]{:S(2)}) collective-permute-start(f32[256]{0:T(256)S(1)} %fusion.84), channel_id=1, source_target_pairs={{0,2},{1,3},{2,4},{3,5},{4,6},{5,7},{6,8},{7,9},{8,10},{9,11},{10,... | collective-permute-start | bytes 3080 | tf_op jit(solution)/shard_map/while/body/eval_jaxpr/ppermute | solution.py:21
  214.0 10.6 %collective-permute-start.3 = (f32[256]{0:T(256)S(1)}, f32[256]{0:T(256)S(1)}, u32[]{:S(2)}, u32[]{:S(2)}) collective-permute-start(f32[256]{0:T(256)S(1)} %fusion.85), channel_id=1, source_target_pairs={{2,0},{3,1},{4,2},{5,3},{6,4},{7,5},{8,6},{9,7},{10,8},{11,9},{12,... | collective-permute-start | bytes 3080 | tf_op jit(solution)/shard_map/while/body/eval_jaxpr/ppermute | solution.py:21
  262.4 24.4 %collective-permute-start = (f32[256]{0:T(256)S(1)}, f32[256]{0:T(256)S(1)}, u32[]{:S(2)}, u32[]{:S(2)}) collective-permute-start(f32[256]{0:T(256)S(1)} %fusion.82), channel_id=1, source_target_pairs={{0,1},{1,2},{2,3},{3,4},{4,5},{5,6},{6,7},{7,8},{8,9},{9,10},{10,1... | collective-permute-start | bytes 3080 | tf_op jit(solution)/shard_map/while/body/eval_jaxpr/ppermute | solution.py:21
  264.9 21.8 %collective-permute-start.1 = (f32[256]{0:T(256)S(1)}, f32[256]{0:T(256)S(1)}, u32[]{:S(2)}, u32[]{:S(2)}) collective-permute-start(f32[256]{0:T(256)S(1)} %fusion.83), channel_id=1, source_target_pairs={{1,0},{2,1},{3,2},{4,3},{5,4},{6,5},{7,6},{8,7},{9,8},{10,9},{11,1... | collective-permute-start | bytes 3080 | tf_op jit(solution)/shard_map/while/body/eval_jaxpr/ppermute | solution.py:21
  274.6 12.1 %collective-permute-start.2 = (f32[256]{0:T(256)S(1)}, f32[256]{0:T(256)S(1)}, u32[]{:S(2)}, u32[]{:S(2)}) collective-permute-start(f32[256]{0:T(256)S(1)} %fusion.84), channel_id=1, source_target_pairs={{0,2},{1,3},{2,4},{3,5},{4,6},{5,7},{6,8},{7,9},{8,10},{9,11},{10,... | collective-permute-start | bytes 3080 | tf_op jit(solution)/shard_map/while/body/eval_jaxpr/ppermute | solution.py:21
  277.2 10.6 %collective-permute-start.3 = (f32[256]{0:T(256)S(1)}, f32[256]{0:T(256)S(1)}, u32[]{:S(2)}, u32[]{:S(2)}) collective-permute-start(f32[256]{0:T(256)S(1)} %fusion.85), channel_id=1, source_target_pairs={{2,0},{3,1},{4,2},{5,3},{6,4},{7,5},{8,6},{9,7},{10,8},{11,9},{12,... | collective-permute-start | bytes 3080 | tf_op jit(solution)/shard_map/while/body/eval_jaxpr/ppermute | solution.py:21
  325.5 24.4 %collective-permute-start = (f32[256]{0:T(256)S(1)}, f32[256]{0:T(256)S(1)}, u32[]{:S(2)}, u32[]{:S(2)}) collective-permute-start(f32[256]{0:T(256)S(1)} %fusion.82), channel_id=1, source_target_pairs={{0,1},{1,2},{2,3},{3,4},{4,5},{5,6},{6,7},{7,8},{8,9},{9,10},{10,1... | collective-permute-start | bytes 3080 | tf_op jit(solution)/shard_map/while/body/eval_jaxpr/ppermute | solution.py:21
  328.1 21.8 %collective-permute-start.1 = (f32[256]{0:T(256)S(1)}, f32[256]{0:T(256)S(1)}, u32[]{:S(2)}, u32[]{:S(2)}) collective-permute-start(f32[256]{0:T(256)S(1)} %fusion.83), channel_id=1, source_target_pairs={{1,0},{2,1},{3,2},{4,3},{5,4},{6,5},{7,6},{8,7},{9,8},{10,9},{11,1... | collective-permute-start | bytes 3080 | tf_op jit(solution)/shard_map/while/body/eval_jaxpr/ppermute | solution.py:21
  337.8 12.1 %collective-permute-start.2 = (f32[256]{0:T(256)S(1)}, f32[256]{0:T(256)S(1)}, u32[]{:S(2)}, u32[]{:S(2)}) collective-permute-start(f32[256]{0:T(256)S(1)} %fusion.84), channel_id=1, source_target_pairs={{0,2},{1,3},{2,4},{3,5},{4,6},{5,7},{6,8},{7,9},{8,10},{9,11},{10,... | collective-permute-start | bytes 3080 | tf_op jit(solution)/shard_map/while/body/eval_jaxpr/ppermute | solution.py:21
  340.4 10.6 %collective-permute-start.3 = (f32[256]{0:T(256)S(1)}, f32[256]{0:T(256)S(1)}, u32[]{:S(2)}, u32[]{:S(2)}) collective-permute-start(f32[256]{0:T(256)S(1)} %fusion.85), channel_id=1, source_target_pairs={{2,0},{3,1},{4,2},{5,3},{6,4},{7,5},{8,6},{9,7},{10,8},{11,9},{12,... | collective-permute-start | bytes 3080 | tf_op jit(solution)/shard_map/while/body/eval_jaxpr/ppermute | solution.py:21
  388.0 20.2 %copy-start = (f32[1024]{0:T(1024)}, f32[1024]{0:T(1024)S(1)}, u32[]{:S(2)}) copy-start(f32[1024]{0:T(1024)S(1)} %get-tuple-element.135) | copy-start | bytes 12292
  388.0 20.2 %copy-start.5 = (f32[1024]{0:T(1024)}, f32[1024]{0:T(1024)S(1)}, u32[]{:S(2)}) copy-start(f32[1024]{0:T(1024)S(1)} %get-tuple-element.136) | copy-start | bytes 12292
  388.1 29.1 %collective-permute-start.5 = (f32[256]{0:T(256)S(1)}, f32[256]{0:T(256)S(1)}, u32[]{:S(2)}, u32[]{:S(2)}) collective-permute-start(f32[256]{0:T(256)S(1)} %fusion.55), channel_id=1, source_target_pairs={{1,0},{2,1},{3,2},{4,3},{5,4},{6,5},{7,6},{8,7},{9,8},{10,9},{11,1... | collective-permute-start | bytes 3080 | tf_op jit(solution)/shard_map/ppermute | solution.py:21
  390.7 28.5 %collective-permute-start.6 = (f32[256]{0:T(256)S(1)}, f32[256]{0:T(256)S(1)}, u32[]{:S(2)}, u32[]{:S(2)}) collective-permute-start(f32[256]{0:T(256)S(1)} %fusion.54), channel_id=1, source_target_pairs={{0,2},{1,3},{2,4},{3,5},{4,6},{5,7},{6,8},{7,9},{8,10},{9,11},{10,... | collective-permute-start | bytes 3080 | tf_op jit(solution)/shard_map/ppermute | solution.py:21
  393.2 35.3 %collective-permute-start.7 = (f32[256]{0:T(256)S(1)}, f32[256]{0:T(256)S(1)}, u32[]{:S(2)}, u32[]{:S(2)}) collective-permute-start(f32[256]{0:T(256)S(1)} %fusion.53), channel_id=1, source_target_pairs={{2,0},{3,1},{4,2},{5,3},{6,4},{7,5},{8,6},{9,7},{10,8},{11,9},{12,... | collective-permute-start | bytes 3080 | tf_op jit(solution)/shard_map/ppermute | solution.py:21
  405.7 59.9 %collective-permute-start.8 = (f32[40,256]{1,0:T(8,128)S(1)}, f32[40,256]{1,0:T(8,128)S(1)}, u32[]{:S(2)}, u32[]{:S(2)}) collective-permute-start(f32[40,256]{1,0:T(8,128)S(1)} %copy_bitcast_fusion.4), channel_id=1, source_target_pairs={{0,1},{1,2},{2,3},{3,4},{4,5},{5,6},{6,7},{7,8},{8,9},{9,10},{10,1... | collective-permute-start | bytes 122888 | tf_op jit(solution)/shard_map/ppermute | solution.py:21
  408.3 57.3 %collective-permute-start.9 = (f32[40,256]{1,0:T(8,128)S(1)}, f32[40,256]{1,0:T(8,128)S(1)}, u32[]{:S(2)}, u32[]{:S(2)}) collective-permute-start(f32[40,256]{1,0:T(8,128)S(1)} %copy_bitcast_fusion.3), channel_id=1, source_target_pairs={{1,0},{2,1},{3,2},{4,3},{5,4},{6,5},{7,6},{8,7},{9,8},{10,9},{11,1... | collective-permute-start | bytes 122888 | tf_op jit(solution)/shard_map/ppermute | solution.py:21
  417.2 48.5 %collective-permute-start.10 = (f32[40,256]{1,0:T(8,128)S(1)}, f32[40,256]{1,0:T(8,128)S(1)}, u32[]{:S(2)}, u32[]{:S(2)}) collective-permute-start(f32[40,256]{1,0:T(8,128)S(1)} %copy_bitcast_fusion.2), channel_id=1, source_target_pairs={{0,2},{1,3},{2,4},{3,5},{4,6},{5,7},{6,8},{7,9},{8,10},{9,11},{10,... | collective-permute-start | bytes 122888 | tf_op jit(solution)/shard_map/ppermute | solution.py:21
  419.1 46.5 %collective-permute-start.11 = (f32[40,256]{1,0:T(8,128)S(1)}, f32[40,256]{1,0:T(8,128)S(1)}, u32[]{:S(2)}, u32[]{:S(2)}) collective-permute-start(f32[40,256]{1,0:T(8,128)S(1)} %copy_bitcast_fusion.1), channel_id=1, source_target_pairs={{2,0},{3,1},{4,2},{5,3},{6,4},{7,5},{8,6},{9,7},{10,8},{11,9},{12,... | collective-permute-start | bytes 122888 | tf_op jit(solution)/shard_map/ppermute | solution.py:21
  484.9 4.0 copy-start.8
where the time goes:
time: 497 us; the launch traced here: 496 us
  local copies, waits for them, and re-layouts  303 us (61%)
  starting transfers between devices  171 us (34%)
  other arithmetic  13.1 us (3%)
  waiting for transfers between devices  6.37 us (1%)
    gather x36, local copies, waits for them, and re-layouts, substep(): jnp.take(extended, neighbours[column]) - height  221 us
    ppermute x32, starting transfers between devices, from_behind(): return lax.ppermute(value, axis, pairs)  171 us
    gather x6, local copies, waits for them, and re-layouts, shards(): near_levels = jnp.take(ext_levels, index)  36.9 us
    gather x6, local copies, waits for them, and re-layouts, shards(): near_tracer = jnp.take(ext_tracer, index, axis=1)  22.8 us
    gather x32, local copies, waits for them, and re-layouts, outgoing(): chosen = jnp.take(blocks, picked_row, axis=-2) * filled_row[:, None]  17.8 us
  transfers between devices with their start and end apart: 32, of which 6 were waited for; matrix products, arithmetic and copies ran while one was open for 57% of the time, Pallas kernels for 0%

commit v1 on v0

v1 whole, which is shorter than its diff:
```python
import functools

import jax
import jax.numpy as jnp
from jax import lax
from jax.experimental import pallas as pl
from jax.experimental.pallas import tpu as pltpu
from jax.sharding import PartitionSpec as P

BLOCK = 128
ROWS = 8
LEV = 40
GROUPS = LEV // 8
SUBSTEPS = 6
OFFSETS = (1, -1, 2, -2)
horizontal_rate = 0.5
vertical_rate = 0.5
tracer_step = 0.2
barotropic_step = 0.5
friction = 0.05


def along(values, index, axis):
    return jnp.take_along_axis(values, index, axis=axis, mode="promise_in_bounds")


def cols(block):
    return pl.ds(block * BLOCK, BLOCK)


def kernel(
    parts, tracer_hbm, bottom_hbm, near_hbm, weight_hbm, ssh_hbm, velocity_hbm, slots, thickness, profile,
    tracer_out, ssh_out, velocity_out,
    tracer_v, bottom_v, near_v, weight_v, ssh_v, velocity_v, result_v,
    send_tracer, halo_tracer, send_level, halo_level, send_height, halo_height,
    near_row, near_lane, weight_s, near_level, forcing_v, summed_v,
    copy_sem, tracer_send, tracer_recv, level_send, level_recv, height_send, height_recv, out_sem,
):
    me = lax.axis_index("dom")

    def start(source, target, number):
        copy = pltpu.make_async_copy(source, target, copy_sem.at[number])
        copy.start()
        return copy

    ssh_copy = start(ssh_hbm, ssh_v, 0)
    bottom_copy = start(bottom_hbm, bottom_v, 1)
    near_copy = start(near_hbm, near_v, 2)
    weight_copy = start(weight_hbm, weight_v, 3)
    tracer_copy = start(tracer_hbm, tracer_v, 4)
    velocity_copy = start(velocity_hbm, velocity_v, 5)

    def to_exists(number):
        target = me + OFFSETS[number]
        return (target >= 0) & (target < parts)

    def from_exists(number):
        source = me - OFFSETS[number]
        return (source >= 0) & (source < parts)

    barrier = pltpu.get_barrier_semaphore()
    for number in range(4):
        @pl.when(to_exists(number))
        def _(number=number):
            pl.semaphore_signal(barrier, inc=1, device_id=(me + OFFSETS[number],), device_id_type=pl.DeviceIdType.MESH)

    row_id = lax.broadcasted_iota(jnp.int32, (ROWS, BLOCK), 0)
    zero = jnp.zeros((ROWS, BLOCK), jnp.float32)
    chosen = zero.astype(jnp.int32)
    for number in range(4):
        for slot in range(2):
            chosen = jnp.where(row_id == 2 * number + slot, slots[0, slot, number], chosen)
    living = jnp.where(chosen >= 0, 1.0, 0.0)
    picked = jnp.maximum(chosen, 0)
    for number in range(4):
        @pl.when(jnp.logical_not(from_exists(number)))
        def _(number=number):
            halo_level[number] = jnp.zeros((2, BLOCK), jnp.float32)
            halo_tracer[number] = jnp.zeros((2, LEV, BLOCK), jnp.float32)
            for step in range(SUBSTEPS):
                halo_height[step, number] = jnp.zeros((2, BLOCK), jnp.float32)

    ssh_copy.wait()
    bottom_copy.wait()
    height = ssh_v[...]
    levels = bottom_v[...].astype(jnp.float32)
    sent = along(levels, picked, 0) * living
    first = along(height, picked, 0) * living
    for number in range(4):
        send_height[0, number] = first[2 * number:2 * number + 2]
        send_level[number] = sent[2 * number:2 * number + 2]

    def height_copy(step, number):
        return pltpu.make_async_remote_copy(
            src_ref=send_height.at[step, number], dst_ref=halo_height.at[step, number],
            send_sem=height_send.at[step, number], recv_sem=height_recv.at[step, number],
            device_id=(me + OFFSETS[number],), device_id_type=pl.DeviceIdType.MESH)

    def level_copy(number):
        return pltpu.make_async_remote_copy(
            src_ref=send_level.at[number], dst_ref=halo_level.at[number],
            send_sem=level_send.at[number], recv_sem=level_recv.at[number],
            device_id=(me + OFFSETS[number],), device_id_type=pl.DeviceIdType.MESH)

    def field_copy(number):
        return pltpu.make_async_remote_copy(
            src_ref=send_tracer.at[number], dst_ref=halo_tracer.at[number],
            send_sem=tracer_send.at[number], recv_sem=tracer_recv.at[number],
            device_id=(me + OFFSETS[number],), device_id_type=pl.DeviceIdType.MESH)

    def when_sending(action):
        for number in range(4):
            @pl.when(to_exists(number))
            def _(number=number):
                action(number)

    def when_receiving(action):
        for number in range(4):
            @pl.when(from_exists(number))
            def _(number=number):
                action(number)

    pl.semaphore_wait(barrier, sum(to_exists(number).astype(jnp.int32) for number in range(4)))
    when_sending(lambda number: height_copy(0, number).start())
    when_sending(lambda number: level_copy(number).start())

    tracer_copy.wait()
    for place in range(ROWS):
        which = jnp.broadcast_to(chosen[place:place + 1], (8, BLOCK))
        for group in range(GROUPS):
            piece = zero
            for block in range(ROWS):
                piece = jnp.where(which == block, tracer_v[pl.ds(group * 8, 8), cols(block)], piece)
            send_tracer[place // 2, place % 2, pl.ds(group * 8, 8), :] = piece
    when_sending(lambda number: field_copy(number).start())

    near_copy.wait()
    weight_copy.wait()
    total_weight = zero
    for column in range(6):
        for block in range(ROWS):
            near_row[column, block:block + 1] = near_v[column:column + 1, cols(block)]
            weight_s[column, block:block + 1] = weight_v[column:column + 1, cols(block)]
    for column in range(6):
        index = near_row[column]
        near_lane[column] = index & (BLOCK - 1)
        near_row[column] = index >> 7
        total_weight = total_weight + weight_s[column]

    def gather_rows(rows, first_row, sums):
        sums = list(sums)
        spread = [jnp.broadcast_to(rows[r:r + 1], (ROWS, BLOCK)) for r in range(ROWS)]
        for column in range(6):
            lane = near_lane[column]
            row = near_row[column]
            for r in range(ROWS):
                sums[column] = jnp.where(row == first_row + r, along(spread[r], lane, 1), sums[column])
        return sums

    def halo_rows(ref, *lead):
        return jnp.concatenate([ref[(*lead, number)] for number in range(4)], axis=0)

    level_id = lax.broadcasted_iota(jnp.int32, (8, BLOCK), 0)
    thick, shape = [], []
    for group in range(GROUPS):
        t, p = zero, zero
        for k in range(8):
            t = jnp.where(level_id == k, thickness[group * 8 + k], t)
            p = jnp.where(level_id == k, profile[group * 8 + k], p)
        thick.append(t)
        shape.append(p)
    level_f = level_id.astype(jnp.float32)
    for block in range(ROWS):
        own = jnp.broadcast_to(levels[block:block + 1], (8, BLOCK))
        top, bottom = zero, zero
        for group in range(GROUPS):
            layer = jnp.where(level_f + float(group * 8) < own, thick[group], 0.0)
            top = top + layer * tracer_v[pl.ds(group * 8, 8), cols(block)]
            bottom = bottom + layer
        forcing_v[block:block + 1] = jnp.sum(top, axis=0, keepdims=True) / jnp.sum(bottom, axis=0, keepdims=True)
    forcing = forcing_v[...]
    velocity_copy.wait()
    speed = velocity_v[...]

    def tracer_block(block, carry):
        at = pl.ds(pl.multiple_of(block * BLOCK, BLOCK), BLOCK)
        fields = [tracer_v[pl.ds(group * 8, 8), at] for group in range(GROUPS)]
        own = jnp.broadcast_to(bottom_v[pl.ds(block, 1), :].astype(jnp.float32), (8, BLOCK))
        sums = [zero] * GROUPS
        for column in range(6):
            index = jnp.broadcast_to(near_v[column:column + 1, at], (8, BLOCK))
            weight = jnp.broadcast_to(weight_v[column:column + 1, at], (8, BLOCK))
            depth = jnp.broadcast_to(near_level[column, pl.ds(block, 1), :], (8, BLOCK))
            lane = index & (BLOCK - 1)
            row = index >> 7
            got = [zero] * GROUPS
            for r in range(2 * ROWS):
                here = row == r
                for group in range(GROUPS):
                    if r < ROWS:
                        table = tracer_v[pl.ds(group * 8, 8), cols(r)]
                    else:
                        table = halo_tracer[(r - ROWS) // 2, (r - ROWS) % 2, pl.ds(group * 8, 8), :]
                    got[group] = jnp.where(here, along(table, lane, 1), got[group])
            for group in range(GROUPS):
                wet = jnp.where(level_f + float(group * 8) < depth, weight, 0.0)
                sums[group] = sums[group] + wet * (got[group] - fields[group])
        for group in range(GROUPS):
            here = fields[group]
            k = level_f + float(group * 8)
            down = jnp.concatenate([here[1:], fields[group + 1][:1] if group < GROUPS - 1 else here[7:]], axis=0)
            up = jnp.concatenate([fields[group - 1][7:] if group else here[:1], here[:7]], axis=0)
            vertical = jnp.where(k + 1.0 < own, down - here, 0.0) + (up - here)
            tendency = horizontal_rate * sums[group] + vertical_rate * vertical
            result_v[pl.ds(group * 8, 8), at] = here + jnp.where(k < own, tracer_step * tendency, 0.0)
        return carry

    summed = zero
    for step in range(SUBSTEPS):
        if step == 1:
            when_receiving(lambda number: field_copy(number).wait_recv())
        if 1 <= step <= 4:
            lax.fori_loop(2 * (step - 1), 2 * step, tracer_block, 0)
        sums = gather_rows(height, 0, [zero] * 6)
        when_receiving(lambda number: height_copy(step, number).wait_recv())
        sums = gather_rows(halo_rows(halo_height, step), ROWS, sums)
        laplace = -total_weight * height
        for column in range(6):
            laplace = laplace + weight_s[column] * sums[column]
        speed = (1.0 - friction) * speed + barotropic_step * (laplace + forcing)
        height = height + barotropic_step * speed
        summed = summed + speed
        if step < SUBSTEPS - 1:
            following = along(height, picked, 0) * living
            for number in range(4):
                send_height[step + 1, number] = following[2 * number:2 * number + 2]
            when_sending(lambda number: height_copy(step + 1, number).start())
        if step == 0:
            when_receiving(lambda number: level_copy(number).wait_recv())
            depths = gather_rows(levels, 0, [zero] * 6)
            depths = gather_rows(halo_rows(halo_level), ROWS, depths)
            for column in range(6):
                near_level[column] = depths[column]

    ssh_v[...] = height
    velocity_v[...] = speed
    ssh_back = pltpu.make_async_copy(ssh_v, ssh_out, out_sem.at[0])
    velocity_back = pltpu.make_async_copy(velocity_v, velocity_out, out_sem.at[1])
    ssh_back.start()
    velocity_back.start()
    mean = summed * (1.0 / SUBSTEPS)
    for block in range(ROWS):
        own = jnp.broadcast_to(levels[block:block + 1], (8, BLOCK))
        push = jnp.broadcast_to(mean[block:block + 1], (8, BLOCK))
        for group in range(GROUPS):
            at = (pl.ds(group * 8, 8), cols(block))
            result_v[at] = result_v[at] + jnp.where(level_f + float(group * 8) < own, shape[group] * push, 0.0)
    back = pltpu.make_async_copy(result_v, tracer_out, out_sem.at[2])
    back.start()
    for step in range(SUBSTEPS):
        when_sending(lambda number: height_copy(step, number).wait_send())
    when_sending(lambda number: level_copy(number).wait_send())
    when_sending(lambda number: field_copy(number).wait_send())
    ssh_back.wait()
    velocity_back.wait()
    back.wait()


def solution(mesh):
    parts = mesh.shape["dom"]

    def shards(tracer, bottom, near, weight, ssh, velocity, slots, thickness, profile):
        hbm = pl.BlockSpec(memory_space=pltpu.HBM)
        smem = pl.BlockSpec(memory_space=pltpu.SMEM)
        tile = (ROWS, BLOCK)
        f32 = jnp.float32
        wide = (LEV, ROWS * BLOCK)
        out = pl.pallas_call(
            functools.partial(kernel, parts),
            out_shape=(jax.ShapeDtypeStruct(wide, f32), jax.ShapeDtypeStruct(tile, f32), jax.ShapeDtypeStruct(tile, f32)),
            in_specs=[hbm] * 6 + [smem] * 3,
            out_specs=(hbm, hbm, hbm),
            scratch_shapes=[
                pltpu.VMEM(wide, f32), pltpu.VMEM(tile, jnp.int32), pltpu.VMEM((6, ROWS * BLOCK), jnp.int32),
                pltpu.VMEM((6, ROWS * BLOCK), f32), pltpu.VMEM(tile, f32), pltpu.VMEM(tile, f32), pltpu.VMEM(wide, f32),
                pltpu.VMEM((4, 2, LEV, BLOCK), f32), pltpu.VMEM((4, 2, LEV, BLOCK), f32),
                pltpu.VMEM((4, 2, BLOCK), f32), pltpu.VMEM((4, 2, BLOCK), f32),
                pltpu.VMEM((SUBSTEPS, 4, 2, BLOCK), f32), pltpu.VMEM((SUBSTEPS, 4, 2, BLOCK), f32),
                pltpu.VMEM((6, *tile), jnp.int32), pltpu.VMEM((6, *tile), jnp.int32), pltpu.VMEM((6, *tile), f32),
                pltpu.VMEM((6, *tile), f32), pltpu.VMEM(tile, f32), pltpu.VMEM(tile, f32),
                pltpu.SemaphoreType.DMA((6,)),
                pltpu.SemaphoreType.DMA((4,)), pltpu.SemaphoreType.DMA((4,)),
                pltpu.SemaphoreType.DMA((4,)), pltpu.SemaphoreType.DMA((4,)),
                pltpu.SemaphoreType.DMA((SUBSTEPS, 4)), pltpu.SemaphoreType.DMA((SUBSTEPS, 4)),
                pltpu.SemaphoreType.DMA((3,)),
            ],
            compiler_params=pltpu.CompilerParams(collective_id=0, has_side_effects=True),
        )(tracer, bottom.reshape(tile), near, weight, ssh.reshape(tile), velocity.reshape(tile), jnp.transpose(slots, (0, 2, 1)), thickness, profile)
        return out[0], out[1].reshape(-1), out[2].reshape(-1)

    placed = (P(None, "dom"), P("dom"), P(None, "dom"), P(None, "dom"), P("dom"), P("dom"), P("dom", None, None), P(), P())
    return jax.shard_map(shards, mesh=mesh, in_specs=placed, out_specs=(P(None, "dom"), P("dom"), P("dom")), check_vma=False)
```

time: 497 us -> 46 us (0.09)
  the two profiles are of different devices: /device:TPU:256 before, /device:TPU:384 now
where the time goes in v1:
time: 46 us; the launch traced here: 45.8 us
  Pallas kernels  42.3 us (92%)
  local copies, waits for them, and re-layouts  2.87 us (6%)
  between operations  0.65 us (1%)
    pallas_call x1, Pallas kernels, shards(): pl.pallas_call(functools.partial(kernel, parts), out_shape=(jax.ShapeDtyp...  42.3 us
    unnamed x7, local copies, waits for them, and re-layouts  2.87 us

profile of v1, /device:TPU:384, one launch (start us, length us, event | category | flops | bytes accessed | tf_op | source)
XLA Modules:
  0.0 45.8 jit_solution(14614460456290728774)
XLA Ops:
  0.6 42.3 %shard_map.112 = (f32[40,1024]{1,0:T(8,128)}, f32[8,128]{1,0:T(8,128)}, f32[8,128]{1,0:T(8,128)}) custom-call(f32[40,1024]{1,0:T(8,128)} %tracer_hbm.1, s32[8,128]{1,0:T(8,128)} %bitcast.6, s32[6,1024]{1,0:T(8,128)} %near_hbm.1, f32[6,1024]{1,0:T(8,128)} %weight_hbm.1, f32[8,128]{1,0:T(8,128)} %bitcast.7, f32[8,128]{1,0:T(8,128)} %bitcast.8, ...), custom_call_target="tpu_custom_call" | custom-call | tf_op jit(solution)/shard_map/pallas_call | solution.py:278
  42.9 0.0 copy-start.1
  42.9 1.6 %copy.15 = f32[40,1024]{1,0:T(8,128)} copy(f32[40,1024]{1,0:T(8,128)} %get-tuple-element.12) | data formatting | bytes 327680
  44.5 0.0 copy-done.1
  44.5 0.0 copy-start
  44.5 0.6 %copy.16 = f32[1024]{0:T(1024)} copy(f32[1024]{0:T(1024)S(1)} %bitcast.10) | data formatting | bytes 8192
  45.1 0.1 copy-done
  45.2 0.6 %copy.17 = f32[1024]{0:T(1024)} copy(f32[1024]{0:T(1024)S(1)} %bitcast.9) | data formatting | bytes 8192
Async XLA Ops:
  42.9 1.6 %copy-start.1 = (f32[8,128]{1,0:T(8,128)S(1)}, f32[8,128]{1,0:T(8,128)}, u32[]{:S(2)}) copy-start(f32[8,128]{1,0:T(8,128)} %get-tuple-element.7) | copy-start | bytes 12292
  44.5 0.7 %copy-start = (f32[8,128]{1,0:T(8,128)S(1)}, f32[8,128]{1,0:T(8,128)}, u32[]{:S(2)}) copy-start(f32[8,128]{1,0:T(8,128)} %get-tuple-element.8) | copy-start | bytes 12292

commit v2 on v1

v2 whole, which is shorter than its diff:
```python
import functools

import jax
import jax.numpy as jnp
from jax import lax
from jax.experimental import pallas as pl
from jax.experimental.pallas import tpu as pltpu
from jax.sharding import PartitionSpec as P

BLOCK = 128
ROWS = 8
LEV = 40
GROUPS = LEV // 8
SUBSTEPS = 6
OFFSETS = (1, -1, 2, -2)
horizontal_rate = 0.5
vertical_rate = 0.5
tracer_step = 0.2
barotropic_step = 0.5
friction = 0.05


FAR = (3, -3, 4, -4)
PLACE = (0, 2, 1, 3)
FAR_ROWS = ((0, 2), (2, 4), (1, 2), (3, 4))
ROUNDS = SUBSTEPS // 2
LAND = 2 * ROWS * BLOCK
TILE = (ROWS, BLOCK)


def along(values, index, axis):
    return jnp.take_along_axis(values, index, axis=axis, mode="promise_in_bounds")


def cols(block):
    return pl.ds(block * BLOCK, BLOCK)


def spread(row):
    return jnp.broadcast_to(row, TILE)


def kernel(
    parts, tracer_hbm, bottom_hbm, near_hbm, weight_hbm, ssh_hbm, velocity_hbm, slots, thickness,
    base_out, tail_out,
    tracer_v, bottom_v, near_v, weight_v, ssh_v, velocity_v, base_v, tail_v,
    send_tracer, halo_tracer, send_level, halo_level, send_chosen, halo_chosen,
    send_near, halo_near, send_weight, halo_weight,
    send_height, halo_height, send_picked, halo_three, halo_four, send_push, halo_push,
    near_row, near_lane, weight_s, near_level, forcing_v,
    copy_sem, out_sem, tracer_sem, level_sem, chosen_sem, near_sem, weight_sem, height_sem, far_sem, push_sem,
):
    me = lax.axis_index("dom")

    def start(source, target, number):
        copy = pltpu.make_async_copy(source, target, copy_sem.at[number])
        copy.start()
        return copy

    tracer_copy = start(tracer_hbm, tracer_v, 4)
    bottom_copy = start(bottom_hbm, bottom_v, 1)
    near_copy = start(near_hbm, near_v, 2)
    weight_copy = start(weight_hbm, weight_v, 3)
    ssh_copy = start(ssh_hbm, ssh_v, 0)
    velocity_copy = start(velocity_hbm, velocity_v, 5)

    def inside(place):
        return (place >= 0) & (place < parts)

    barrier = pltpu.get_barrier_semaphore()
    for offset in OFFSETS + FAR:
        @pl.when(inside(me + offset))
        def _(offset=offset):
            pl.semaphore_signal(barrier, inc=1, device_id=(me + offset,), device_id_type=pl.DeviceIdType.MESH)

    row_id = lax.broadcasted_iota(jnp.int32, TILE, 0)
    level_f = row_id.astype(jnp.float32)
    zero = jnp.zeros(TILE, jnp.float32)

    for number in range(4):
        @pl.when(jnp.logical_not(inside(me - OFFSETS[number])))
        def _(number=number):
            halo_chosen[number] = jnp.full(TILE, -1, jnp.int32)
            halo_near[number] = jnp.full((2, *TILE), LAND, jnp.int32)
            halo_weight[number] = jnp.zeros((2, *TILE), jnp.float32)
            halo_level[number] = jnp.zeros((2, BLOCK), jnp.float32)
            halo_tracer[number] = jnp.zeros((2, LEV, BLOCK), jnp.float32)
            for turn in range(ROUNDS):
                halo_height[turn, number] = zero
                halo_push[turn, number] = jnp.zeros((2, BLOCK), jnp.float32)
        @pl.when(jnp.logical_not(inside(me - FAR[number])))
        def _(number=number):
            for turn in range(ROUNDS):
                if number < 2:
                    halo_three[turn, number] = jnp.zeros((2, 2, BLOCK), jnp.float32)
                else:
                    halo_four[turn, number - 2] = jnp.zeros((1, 2, BLOCK), jnp.float32)

    def remote(source, target, sems, offset):
        return pltpu.make_async_remote_copy(
            src_ref=source, dst_ref=target, send_sem=sems.at[0], recv_sem=sems.at[1],
            device_id=(me + offset,), device_id_type=pl.DeviceIdType.MESH)

    def tracer_link(n):
        return remote(send_tracer.at[n], halo_tracer.at[n], tracer_sem.at[n], OFFSETS[n])

    def level_link(n):
        return remote(send_level.at[n], halo_level.at[n], level_sem.at[n], OFFSETS[n])

    def chosen_link(n):
        return remote(send_chosen, halo_chosen.at[n], chosen_sem.at[n], OFFSETS[n])

    def near_link(n):
        return remote(send_near.at[n], halo_near.at[n], near_sem.at[n], OFFSETS[n])

    def weight_link(n):
        return remote(send_weight.at[n], halo_weight.at[n], weight_sem.at[n], OFFSETS[n])

    def height_link(turn, n):
        return remote(send_height.at[turn], halo_height.at[turn, n], height_sem.at[turn, n], OFFSETS[n])

    def push_link(turn, n):
        return remote(send_push.at[turn, n], halo_push.at[turn, n], push_sem.at[turn, n], OFFSETS[n])

    def far_link(turn, n):
        low, high = FAR_ROWS[n]
        target = halo_three.at[turn, n] if n < 2 else halo_four.at[turn, n - 2]
        return remote(send_picked.at[turn, pl.ds(low, high - low)], target, far_sem.at[turn, n], FAR[n])

    def begin(links, offsets=OFFSETS):
        for number in range(4):
            @pl.when(inside(me + offsets[number]))
            def _(number=number):
                for link in links:
                    link(number).start()

    def arrive(links, offsets=OFFSETS):
        for number in range(4):
            @pl.when(inside(me - offsets[number]))
            def _(number=number):
                for link in links:
                    link(number).wait_recv()

    def leave(links, offsets=OFFSETS):
        for number in range(4):
            @pl.when(inside(me + offsets[number]))
            def _(number=number):
                for link in links:
                    link(number).wait_send()

    chosen = zero.astype(jnp.int32)
    for number in range(4):
        for slot in range(2):
            chosen = jnp.where(row_id == 2 * number + slot, slots[0, slot, number], chosen)
    send_chosen[...] = chosen

    def pick(values, choice):
        return jnp.where(choice >= 0, along(values, jnp.maximum(choice, 0), 0), 0.0)

    def put_round(turn, height, push):
        picked = pick(height, chosen)
        pushed = pick(push, chosen)
        send_height[turn] = height
        for number in range(4):
            send_picked[turn, PLACE[number]] = picked[2 * number:2 * number + 2]
            send_push[turn, number] = pushed[2 * number:2 * number + 2]
        return picked

    bottom_copy.wait()
    levels = bottom_v[...].astype(jnp.float32)
    sent_levels = pick(levels, chosen)
    for number in range(4):
        send_level[number] = sent_levels[2 * number:2 * number + 2]
    thick = []
    for group in range(GROUPS):
        t = zero
        for k in range(8):
            t = jnp.where(row_id == k, thickness[group * 8 + k], t)
        thick.append(t)
    tracer_copy.wait()
    for block in range(ROWS):
        own = spread(levels[block:block + 1])
        top, under = zero, zero
        for group in range(GROUPS):
            layer = jnp.where(level_f + float(group * 8) < own, thick[group], 0.0)
            top = top + layer * tracer_v[pl.ds(group * 8, 8), cols(block)]
            under = under + layer
        forcing_v[block:block + 1] = jnp.sum(top, axis=0, keepdims=True) / jnp.sum(under, axis=0, keepdims=True)
    forcing = forcing_v[...]
    ssh_copy.wait()
    velocity_copy.wait()
    height = ssh_v[...]

    def pushed_by(speed):
        return (1.0 - friction) * speed + barotropic_step * forcing

    push = pushed_by(velocity_v[...])
    picked = put_round(0, height, push)

    near_copy.wait()
    weight_copy.wait()
    for place in range(ROWS):
        which = spread(chosen[place:place + 1])
        n, slot = place // 2, place % 2
        index = jnp.full((6, BLOCK), LAND, jnp.int32)
        amount = jnp.zeros((6, BLOCK), jnp.float32)
        for block in range(ROWS):
            index = jnp.where(which[:6] == block, near_v[:, cols(block)], index)
            amount = jnp.where(which[:6] == block, weight_v[:, cols(block)], amount)
        send_near[n, slot] = jnp.full(TILE, LAND, jnp.int32)
        send_weight[n, slot] = zero
        send_near[n, slot, 0:6] = index
        send_weight[n, slot, 0:6] = amount
    total_weight = zero
    for column in range(6):
        for block in range(ROWS):
            near_row[column, block:block + 1] = near_v[column:column + 1, cols(block)]
            weight_s[column, block:block + 1] = weight_v[column:column + 1, cols(block)]
    for column in range(6):
        index = near_row[column]
        near_lane[column] = index & (BLOCK - 1)
        near_row[column] = index >> 7
        total_weight = total_weight + weight_s[column]
    for place in range(ROWS):
        which = spread(chosen[place:place + 1])
        for group in range(GROUPS):
            piece = zero
            for block in range(ROWS):
                piece = jnp.where(which == block, tracer_v[pl.ds(group * 8, 8), cols(block)], piece)
            send_tracer[place // 2, place % 2, pl.ds(group * 8, 8), :] = piece

    pl.semaphore_wait(barrier, sum(inside(me + offset).astype(jnp.int32) for offset in OFFSETS + FAR))
    begin([functools.partial(far_link, 0)], FAR)
    begin([functools.partial(height_link, 0), chosen_link, near_link, weight_link, functools.partial(push_link, 0)])
    begin([level_link, tracer_link])

    def gather(rows, first_row, columns, sums):
        sums = list(sums)
        wide = [spread(rows[r:r + 1]) for r in range(ROWS)]
        for i, (row, lane) in enumerate(columns):
            for r in range(ROWS):
                sums[i] = jnp.where(row == first_row + r, along(wide[r], lane, 1), sums[i])
        return sums

    def own_columns():
        return [(near_row[column], near_lane[column]) for column in range(6)]

    def own_update(sums, height, push):
        laplace = -total_weight * height
        for column in range(6):
            laplace = laplace + weight_s[column] * sums[column]
        speed = push + barotropic_step * laplace
        return speed, height + barotropic_step * speed

    def tracer_block(block, carry):
        at = pl.ds(pl.multiple_of(block * BLOCK, BLOCK), BLOCK)
        fields = [tracer_v[pl.ds(group * 8, 8), at] for group in range(GROUPS)]
        own = spread(bottom_v[pl.ds(block, 1), :].astype(jnp.float32))
        sums = [zero] * GROUPS
        for column in range(6):
            index = spread(near_v[column:column + 1, at])
            weight = spread(weight_v[column:column + 1, at])
            depth = spread(near_level[column, pl.ds(block, 1), :])
            lane = index & (BLOCK - 1)
            row = index >> 7
            got = [zero] * GROUPS
            for r in range(2 * ROWS):
                here = row == r
                for group in range(GROUPS):
                    if r < ROWS:
                        table = tracer_v[pl.ds(group * 8, 8), cols(r)]
                    else:
                        table = halo_tracer[(r - ROWS) // 2, (r - ROWS) % 2, pl.ds(group * 8, 8), :]
                    got[group] = jnp.where(here, along(table, lane, 1), got[group])
            for group in range(GROUPS):
                wet = jnp.where(level_f + float(group * 8) < depth, weight, 0.0)
                sums[group] = sums[group] + wet * (got[group] - fields[group])
        for group in range(GROUPS):
            here = fields[group]
            k = level_f + float(group * 8)
            down = jnp.concatenate([here[1:], fields[group + 1][:1] if group < GROUPS - 1 else here[7:]], axis=0)
            up = jnp.concatenate([fields[group - 1][7:] if group else here[:1], here[:7]], axis=0)
            vertical = jnp.where(k + 1.0 < own, down - here, 0.0) + (up - here)
            tendency = horizontal_rate * sums[group] + vertical_rate * vertical
            base_v[pl.ds(group * 8, 8), at] = here + jnp.where(k < own, tracer_step * tendency, 0.0)
        return carry

    base_copy = pltpu.make_async_copy(base_v, base_out, out_sem.at[0])
    summed = zero
    for turn in range(ROUNDS):
        if turn == 1:
            arrive([tracer_link])
        if turn >= 1:
            lax.fori_loop(4 * (turn - 1), 4 * turn, tracer_block, 0)
        if turn == ROUNDS - 1:
            base_copy.start()
        sums = gather(height, 0, own_columns(), [zero] * 6)
        if turn == 0:
            arrive([functools.partial(height_link, turn), chosen_link])
        else:
            arrive([functools.partial(height_link, turn)])
        fields = [halo_height[turn, n] for n in range(4)]
        choices = [halo_chosen[n] for n in range(4)]
        picks = [pick(fields[n], choices[n]) for n in range(4)]
        halo = jnp.concatenate([picks[n][2 * n:2 * n + 2] for n in range(4)], axis=0)
        sums = gather(halo, ROWS, own_columns(), sums)
        arrive([functools.partial(far_link, turn)], FAR)
        if turn == 0:
            arrive([near_link, weight_link])
        arrive([functools.partial(push_link, turn)])
        laplaces = []
        for h in range(4):
            rows = []
            for g in range(4):
                gap = OFFSETS[h] + OFFSETS[g]
                if gap == 0:
                    rows.append(picked[2 * g:2 * g + 2])
                elif gap in OFFSETS:
                    rows.append(picks[OFFSETS.index(gap)][2 * g:2 * g + 2])
                else:
                    f = FAR.index(gap)
                    at = PLACE[g] - FAR_ROWS[f][0]
                    rows.append(halo_three[turn, f, at] if f < 2 else halo_four[turn, f - 2, at])
            around = jnp.concatenate(rows, axis=0)
            indices = [halo_near[h, slot] for slot in range(2)]
            columns = [(index >> 7, index & (BLOCK - 1)) for index in indices]
            found = gather(fields[h], 0, columns, [zero] * 2)
            found = gather(around, ROWS, columns, found)
            for slot in range(2):
                place = 2 * h + slot
                difference = halo_weight[h, slot] * (found[slot] - spread(halo[place:place + 1]))
                laplaces.append(jnp.sum(difference, axis=0, keepdims=True))
        outer = jnp.concatenate([halo_push[turn, n] for n in range(4)], axis=0)
        outer = outer + barotropic_step * jnp.concatenate(laplaces, axis=0)
        alive = jnp.concatenate([choices[n][2 * n:2 * n + 2] for n in range(4)], axis=0)
        halo = jnp.where(alive >= 0, halo + barotropic_step * outer, 0.0)
        speed, height = own_update(sums, height, push)
        push = pushed_by(speed)
        summed = summed + speed

        sums = gather(height, 0, own_columns(), [zero] * 6)
        sums = gather(halo, ROWS, own_columns(), sums)
        speed, height = own_update(sums, height, push)
        push = pushed_by(speed)
        summed = summed + speed
        if turn < ROUNDS - 1:
            picked = put_round(turn + 1, height, push)
            begin([functools.partial(far_link, turn + 1)], FAR)
            begin([functools.partial(height_link, turn + 1), functools.partial(push_link, turn + 1)])
        if turn == 0:
            arrive([level_link])
            depths = gather(levels, 0, own_columns(), [zero] * 6)
            around = jnp.concatenate([halo_level[n] for n in range(4)], axis=0)
            depths = gather(around, ROWS, own_columns(), depths)
            for column in range(6):
                near_level[column] = depths[column]

    tail_v[0] = height
    tail_v[1] = speed
    tail_v[2] = summed * (1.0 / SUBSTEPS)
    tail_copy = pltpu.make_async_copy(tail_v, tail_out, out_sem.at[1])
    tail_copy.start()
    for turn in range(ROUNDS):
        leave([functools.partial(far_link, turn)], FAR)
        leave([functools.partial(height_link, turn), functools.partial(push_link, turn)])
    leave([chosen_link, near_link, weight_link, level_link, tracer_link])
    base_copy.wait()
    tail_copy.wait()


def finish(base_hbm, tail_hbm, bottom_hbm, profile, tracer_out, ssh_out, velocity_out, base_v, tail_v, bottom_v, in_sem, out_sem):
    copies = [
        pltpu.make_async_copy(source, target, in_sem.at[i])
        for i, (source, target) in enumerate(((tail_hbm, tail_v), (bottom_hbm, bottom_v), (base_hbm, base_v)))
    ]
    for copy in copies:
        copy.start()
    backs = [
        pltpu.make_async_copy(source, target, out_sem.at[i])
        for i, (source, target) in enumerate(((tail_v.at[0], ssh_out), (tail_v.at[1], velocity_out), (base_v, tracer_out)))
    ]
    row_id = lax.broadcasted_iota(jnp.int32, TILE, 0)
    shape = []
    for group in range(GROUPS):
        p = jnp.zeros(TILE, jnp.float32)
        for k in range(8):
            p = jnp.where(row_id == k, profile[group * 8 + k], p)
        shape.append(p)
    copies[0].wait()
    backs[0].start()
    backs[1].start()
    copies[1].wait()
    copies[2].wait()
    mean = tail_v[2]
    levels = bottom_v[...]
    for block in range(ROWS):
        own = spread(levels[block:block + 1])
        push = spread(mean[block:block + 1])
        for group in range(GROUPS):
            at = (pl.ds(group * 8, 8), cols(block))
            base_v[at] = base_v[at] + jnp.where(row_id + group * 8 < own, shape[group] * push, 0.0)
    backs[2].start()
    for back in backs:
        back.wait()


def solution(mesh):
    parts = mesh.shape["dom"]

    def shards(tracer, bottom, near, weight, ssh, velocity, slots, thickness, profile):
        hbm = pl.BlockSpec(memory_space=pltpu.HBM)
        smem = pl.BlockSpec(memory_space=pltpu.SMEM)
        f32, i32 = jnp.float32, jnp.int32
        wide = (LEV, ROWS * BLOCK)
        dma = pltpu.SemaphoreType.DMA
        vmem = pltpu.VMEM
        levels = bottom.reshape(TILE)
        base, tail = pl.pallas_call(
            functools.partial(kernel, parts),
            out_shape=(jax.ShapeDtypeStruct(wide, f32), jax.ShapeDtypeStruct((3, *TILE), f32)),
            in_specs=[hbm] * 6 + [smem] * 2,
            out_specs=(hbm, hbm),
            scratch_shapes=[
                vmem(wide, f32), vmem(TILE, i32), vmem((6, ROWS * BLOCK), i32), vmem((6, ROWS * BLOCK), f32),
                vmem(TILE, f32), vmem(TILE, f32), vmem(wide, f32), vmem((3, *TILE), f32),
                vmem((4, 2, LEV, BLOCK), f32), vmem((4, 2, LEV, BLOCK), f32),
                vmem((4, 2, BLOCK), f32), vmem((4, 2, BLOCK), f32), vmem(TILE, i32), vmem((4, *TILE), i32),
                vmem((4, 2, *TILE), i32), vmem((4, 2, *TILE), i32), vmem((4, 2, *TILE), f32), vmem((4, 2, *TILE), f32),
                vmem((ROUNDS, *TILE), f32), vmem((ROUNDS, 4, *TILE), f32),
                vmem((ROUNDS, 4, 2, BLOCK), f32), vmem((ROUNDS, 2, 2, 2, BLOCK), f32), vmem((ROUNDS, 2, 1, 2, BLOCK), f32),
                vmem((ROUNDS, 4, 2, BLOCK), f32), vmem((ROUNDS, 4, 2, BLOCK), f32),
                vmem((6, *TILE), i32), vmem((6, *TILE), i32), vmem((6, *TILE), f32), vmem((6, *TILE), f32), vmem(TILE, f32),
                dma((6,)), dma((2,)), dma((4, 2)), dma((4, 2)), dma((4, 2)), dma((4, 2)), dma((4, 2)),
                dma((ROUNDS, 4, 2)), dma((ROUNDS, 4, 2)), dma((ROUNDS, 4, 2)),
            ],
            compiler_params=pltpu.CompilerParams(collective_id=0, has_side_effects=True),
        )(tracer, levels, near, weight, ssh.reshape(TILE), velocity.reshape(TILE), jnp.transpose(slots, (0, 2, 1)), thickness)
        tile = jax.ShapeDtypeStruct(TILE, f32)
        out = pl.pallas_call(
            finish,
            out_shape=(jax.ShapeDtypeStruct(wide, f32), tile, tile),
            in_specs=[hbm] * 3 + [smem],
            out_specs=(hbm, hbm, hbm),
            scratch_shapes=[vmem(wide, f32), vmem((3, *TILE), f32), vmem(TILE, i32), dma((3,)), dma((3,))],
        )(base, tail, levels, profile)
        return out[0], out[1].reshape(-1), out[2].reshape(-1)

    placed = (P(None, "dom"), P("dom"), P(None, "dom"), P(None, "dom"), P("dom"), P("dom"), P("dom", None, None), P(), P())
    return jax.shard_map(shards, mesh=mesh, in_specs=placed, out_specs=(P(None, "dom"), P("dom"), P("dom")), check_vma=False)
```

time: 46 us -> 29.5 us (0.64)
  Pallas kernels: 42.3 us -> 28.5 us
  local copies, waits for them, and re-layouts: 2.87 us -> 0 us
    pallas_call x1, Pallas kernels: 42.3 us -> 26.2 us  [shards(): pl.pallas_call(functools.partial(kernel, parts), out_shape=(jax.ShapeDtyp...]
    unnamed x7 -> x0, local copies, waits for them, and re-layouts: 2.87 us -> none
    pallas_call x0 -> x1, Pallas kernels: none -> 2.36 us  [shards(): pl.pallas_call(finish, out_shape=(jax.ShapeDtypeStruct(wide, f32), tile,...]
where the time goes in v2:
time: 29.5 us; the launch traced here: 29.2 us
  Pallas kernels  28.5 us (97%)
  between operations  0.64 us (2%)
    pallas_call x1, Pallas kernels, shards(): pl.pallas_call(functools.partial(kernel, parts), out_shape=(jax.ShapeDtyp...  26.2 us
    pallas_call x1, Pallas kernels, shards(): pl.pallas_call(finish, out_shape=(jax.ShapeDtypeStruct(wide, f32), tile,...  2.36 us

profile of v2, /device:TPU:384, one launch (start us, length us, event | category | flops | bytes accessed | tf_op | source)
XLA Modules:
  0.0 29.2 jit_solution(1439018310146697922)
XLA Ops:
  0.6 26.2 %shard_map.112 = (f32[40,1024]{1,0:T(8,128)}, f32[3,8,128]{2,1,0:T(8,128)}) custom-call(f32[40,1024]{1,0:T(8,128)} %tracer_hbm.1, s32[8,128]{1,0:T(8,128)} %bitcast.6, s32[6,1024]{1,0:T(8,128)} %near_hbm.1, f32[6,1024]{1,0:T(8,128)} %weight_hbm.1, f32[8,128]{1,0:T(8,128)} %bitcast.8, f32[8,128]{1,0:T(8,128)} %bitcast.9, s32[1,2,4]{2,1,0:T(2,128)} %bitcast.10, ...), custom_call_target="tpu_custom_call" | custom-call | tf_op jit(solution)/shard_map/pallas_call | solution.py:418
  26.8 2.4 %shard_map.113 = (f32[40,1024]{1,0:T(8,128)}, f32[8,128]{1,0:T(8,128)}, f32[8,128]{1,0:T(8,128)}) custom-call(f32[40,1024]{1,0:T(8,128)} %get-tuple-element.8.base_hbm, f32[3,8,128]{2,1,0:T(8,128)} %get-tuple-element.9.tail_hbm, s32[8,128]{1,0:T(8,128)} %bitcast.7, f32[40]{0:T(128)} %profile.1), custom_call_target="tpu_custom_call" | custom-call | tf_op jit(solution)/shard_map/pallas_call | solution.py:439

commit v3 on v2

--- a/solution.py
+++ b/solution.py
@@ -41,14 +41,14 @@
 
 
 def kernel(
-    parts, tracer_hbm, bottom_hbm, near_hbm, weight_hbm, ssh_hbm, velocity_hbm, slots, thickness,
-    base_out, tail_out,
-    tracer_v, bottom_v, near_v, weight_v, ssh_v, velocity_v, base_v, tail_v,
+    parts, tracer_hbm, bottom_hbm, near_hbm, weight_hbm, ssh_hbm, velocity_hbm, slots_hbm, thickness_hbm, profile_hbm,
+    base_v, tail_v,
+    tracer_v, bottom_v, near_v, weight_v, ssh_v, velocity_v, slots, thickness, profile,
     send_tracer, halo_tracer, send_level, halo_level, send_chosen, halo_chosen,
     send_near, halo_near, send_weight, halo_weight,
     send_height, halo_height, send_picked, halo_three, halo_four, send_push, halo_push,
     near_row, near_lane, weight_s, near_level, forcing_v,
-    copy_sem, out_sem, tracer_sem, level_sem, chosen_sem, near_sem, weight_sem, height_sem, far_sem, push_sem,
+    copy_sem, tracer_sem, level_sem, chosen_sem, near_sem, weight_sem, height_sem, far_sem, push_sem,
 ):
     me = lax.axis_index("dom")
 
@@ -57,21 +57,24 @@
         copy.start()
         return copy
 
+    def inside(place):
+        return (place >= 0) & (place < parts)
+
+    barrier = pltpu.get_barrier_semaphore()
+    for offset in OFFSETS + FAR:
+        @pl.when(inside(me + offset))
+        def _(offset=offset):
+            pl.semaphore_signal(barrier, inc=1, device_id=(me + offset,), device_id_type=pl.DeviceIdType.MESH)
+
+    slots_copy = start(slots_hbm, slots, 6)
+    thickness_copy = start(thickness_hbm, thickness, 7)
+    profile_copy = start(profile_hbm, profile, 8)
     tracer_copy = start(tracer_hbm, tracer_v, 4)
     bottom_copy = start(bottom_hbm, bottom_v, 1)
     near_copy = start(near_hbm, near_v, 2)
     weight_copy = start(weight_hbm, weight_v, 3)
     ssh_copy = start(ssh_hbm, ssh_v, 0)
     velocity_copy = start(velocity_hbm, velocity_v, 5)
-
-    def inside(place):
-        return (place >= 0) & (place < parts)
-
-    barrier = pltpu.get_barrier_semaphore()
-    for offset in OFFSETS + FAR:
-        @pl.when(inside(me + offset))
-        def _(offset=offset):
-            pl.semaphore_signal(barrier, inc=1, device_id=(me + offset,), device_id_type=pl.DeviceIdType.MESH)
 
     row_id = lax.broadcasted_iota(jnp.int32, TILE, 0)
     level_f = row_id.astype(jnp.float32)
@@ -148,6 +151,7 @@
                 for link in links:
                     link(number).wait_send()
 
+    slots_copy.wait()
     chosen = zero.astype(jnp.int32)
     for number in range(4):
         for slot in range(2):
@@ -171,12 +175,17 @@
     sent_levels = pick(levels, chosen)
     for number in range(4):
         send_level[number] = sent_levels[2 * number:2 * number + 2]
+    thickness_copy.wait()
+    profile_copy.wait()
     thick = []
     for group in range(GROUPS):
-        t = zero
+        t, p = zero, zero
         for k in range(8):
             t = jnp.where(row_id == k, thickness[group * 8 + k], t)
+            p = jnp.where(row_id == k, profile[group * 8 + k], p)
         thick.append(t)
+        tail_v[4 + group] = p
+    tail_v[3] = levels
     tracer_copy.wait()
     for block in range(ROWS):
         own = spread(levels[block:block + 1])
@@ -236,9 +245,10 @@
 
     def gather(rows, first_row, columns, sums):
         sums = list(sums)
-        wide = [spread(rows[r:r + 1]) for r in range(ROWS)]
+        count = rows.shape[0]
+        wide = [spread(rows[r:r + 1]) for r in range(count)]
         for i, (row, lane) in enumerate(columns):
-            for r in range(ROWS):
+            for r in range(count):
                 sums[i] = jnp.where(row == first_row + r, along(wide[r], lane, 1), sums[i])
         return sums
 
@@ -285,60 +295,57 @@
             base_v[pl.ds(group * 8, 8), at] = here + jnp.where(k < own, tracer_step * tendency, 0.0)
         return carry
 
-    base_copy = pltpu.make_async_copy(base_v, base_out, out_sem.at[0])
     summed = zero
     for turn in range(ROUNDS):
         if turn == 1:
             arrive([tracer_link])
         if turn >= 1:
             lax.fori_loop(4 * (turn - 1), 4 * turn, tracer_block, 0)
-        if turn == ROUNDS - 1:
-            base_copy.start()
         sums = gather(height, 0, own_columns(), [zero] * 6)
-        if turn == 0:
-            arrive([functools.partial(height_link, turn), chosen_link])
-        else:
-            arrive([functools.partial(height_link, turn)])
+        arrive([functools.partial(height_link, turn)] + ([chosen_link] if turn == 0 else []))
         fields = [halo_height[turn, n] for n in range(4)]
         choices = [halo_chosen[n] for n in range(4)]
         picks = [pick(fields[n], choices[n]) for n in range(4)]
         halo = jnp.concatenate([picks[n][2 * n:2 * n + 2] for n in range(4)], axis=0)
+        alive = jnp.concatenate([choices[n][2 * n:2 * n + 2] for n in range(4)], axis=0)
         sums = gather(halo, ROWS, own_columns(), sums)
-        arrive([functools.partial(far_link, turn)], FAR)
-        if turn == 0:
-            arrive([near_link, weight_link])
-        arrive([functools.partial(push_link, turn)])
-        laplaces = []
+        arrive([functools.partial(push_link, turn)] + ([near_link, weight_link] if turn == 0 else []))
+        outer = jnp.concatenate([halo_push[turn, n] for n in range(4)], axis=0)
+
+        def partner_columns(h):
+            indices = [halo_near[h, slot] for slot in range(2)]
+            return [(index >> 7, index & (BLOCK - 1)) for index in indices]
+
+        found = []
         for h in range(4):
-            rows = []
+            got = gather(fields[h], 0, partner_columns(h), [zero] * 2)
             for g in range(4):
                 gap = OFFSETS[h] + OFFSETS[g]
-                if gap == 0:
-                    rows.append(picked[2 * g:2 * g + 2])
-                elif gap in OFFSETS:
-                    rows.append(picks[OFFSETS.index(gap)][2 * g:2 * g + 2])
-                else:
-                    f = FAR.index(gap)
-                    at = PLACE[g] - FAR_ROWS[f][0]
-                    rows.append(halo_three[turn, f, at] if f < 2 else halo_four[turn, f - 2, at])
-            around = jnp.concatenate(rows, axis=0)
-            indices = [halo_near[h, slot] for slot in range(2)]
-            columns = [(index >> 7, index & (BLOCK - 1)) for index in indices]
-            found = gather(fields[h], 0, columns, [zero] * 2)
-            found = gather(around, ROWS, columns, found)
-            for slot in range(2):
-                place = 2 * h + slot
-                difference = halo_weight[h, slot] * (found[slot] - spread(halo[place:place + 1]))
-                laplaces.append(jnp.sum(difference, axis=0, keepdims=True))
-        outer = jnp.concatenate([halo_push[turn, n] for n in range(4)], axis=0)
-        outer = outer + barotropic_step * jnp.concatenate(laplaces, axis=0)
-        alive = jnp.concatenate([choices[n][2 * n:2 * n + 2] for n in range(4)], axis=0)
-        halo = jnp.where(alive >= 0, halo + barotropic_step * outer, 0.0)
+                if gap == 0 or gap in OFFSETS:
+                    rows = picked if gap == 0 else picks[OFFSETS.index(gap)]
+                    got = gather(rows[2 * g:2 * g + 2], ROWS + 2 * g, partner_columns(h), got)
+            found.append(got)
         speed, height = own_update(sums, height, push)
         push = pushed_by(speed)
         summed = summed + speed
-
         sums = gather(height, 0, own_columns(), [zero] * 6)
+
+        arrive([functools.partial(far_link, turn)], FAR)
+        laplaces = []
+        for h in range(4):
+            for g in range(4):
+                gap = OFFSETS[h] + OFFSETS[g]
+                if gap in FAR:
+                    f = FAR.index(gap)
+                    at = PLACE[g] - FAR_ROWS[f][0]
+                    rows = halo_three[turn, f, at] if f < 2 else halo_four[turn, f - 2, at]
+                    found[h] = gather(rows, ROWS + 2 * g, partner_columns(h), found[h])
+            for slot in range(2):
+                place = 2 * h + slot
+                difference = halo_weight[h, slot] * (found[h][slot] - spread(halo[place:place + 1]))
+                laplaces.append(jnp.sum(difference, axis=0, keepdims=True))
+        outer = outer + barotropic_step * jnp.concatenate(laplaces, axis=0)
+        halo = jnp.where(alive >= 0, halo + barotropic_step * outer, 0.0)
         sums = gather(halo, ROWS, own_columns(), sums)
         speed, height = own_update(sums, height, push)
         push = pushed_by(speed)
@@ -358,48 +365,34 @@
     tail_v[0] = height
     tail_v[1] = speed
     tail_v[2] = summed * (1.0 / SUBSTEPS)
-    tail_copy = pltpu.make_async_copy(tail_v, tail_out, out_sem.at[1])
-    tail_copy.start()
     for turn in range(ROUNDS):
         leave([functools.partial(far_link, turn)], FAR)
         leave([functools.partial(height_link, turn), functools.partial(push_link, turn)])
     leave([chosen_link, near_link, weight_link, level_link, tracer_link])
-    base_copy.wait()
-    tail_copy.wait()
-
-
-def finish(base_hbm, tail_hbm, bottom_hbm, profile, tracer_out, ssh_out, velocity_out, base_v, tail_v, bottom_v, in_sem, out_sem):
-    copies = [
-        pltpu.make_async_copy(source, target, in_sem.at[i])
-        for i, (source, target) in enumerate(((tail_hbm, tail_v), (bottom_hbm, bottom_v), (base_hbm, base_v)))
-    ]
-    for copy in copies:
-        copy.start()
-    backs = [
-        pltpu.make_async_copy(source, target, out_sem.at[i])
-        for i, (source, target) in enumerate(((tail_v.at[0], ssh_out), (tail_v.at[1], velocity_out), (base_v, tracer_out)))
-    ]
-    row_id = lax.broadcasted_iota(jnp.int32, TILE, 0)
-    shape = []
-    for group in range(GROUPS):
-        p = jnp.zeros(TILE, jnp.float32)
-        for k in range(8):
-            p = jnp.where(row_id == k, profile[group * 8 + k], p)
-        shape.append(p)
-    copies[0].wait()
-    backs[0].start()
-    backs[1].start()
-    copies[1].wait()
-    copies[2].wait()
+
+
+def finish(base_v, tail_v, tracer_out, ssh_out, velocity_out, result_v, out_sem):
+    height_back = pltpu.make_async_copy(tail_v.at[0], ssh_out, out_sem.at[ROWS])
+    speed_back = pltpu.make_async_copy(tail_v.at[1], velocity_out, out_sem.at[ROWS + 1])
+    height_back.start()
+    speed_back.start()
     mean = tail_v[2]
-    levels = bottom_v[...]
+    levels = tail_v[3]
+    level_f = lax.broadcasted_iota(jnp.int32, TILE, 0).astype(jnp.float32)
+    shape = [tail_v[4 + group] for group in range(GROUPS)]
+    backs = []
     for block in range(ROWS):
         own = spread(levels[block:block + 1])
         push = spread(mean[block:block + 1])
         for group in range(GROUPS):
             at = (pl.ds(group * 8, 8), cols(block))
-            base_v[at] = base_v[at] + jnp.where(row_id + group * 8 < own, shape[group] * push, 0.0)
-    backs[2].start()
+            result_v[at] = base_v[at] + jnp.where(level_f + float(group * 8) < own, shape[group] * push, 0.0)
+        if block % 4 == 3:
+            half = pl.ds((block - 3) * BLOCK, 4 * BLOCK)
+            backs.append(pltpu.make_async_copy(result_v.at[:, half], tracer_out.at[:, half], out_sem.at[block]))
+            backs[-1].start()
+    height_back.wait()
+    speed_back.wait()
     for back in backs:
         back.wait()
 
@@ -409,20 +402,20 @@
 
     def shards(tracer, bottom, near, weight, ssh, velocity, slots, thickness, profile):
         hbm = pl.BlockSpec(memory_space=pltpu.HBM)
-        smem = pl.BlockSpec(memory_space=pltpu.SMEM)
+        inner = pl.BlockSpec(memory_space=pltpu.VMEM)
         f32, i32 = jnp.float32, jnp.int32
         wide = (LEV, ROWS * BLOCK)
         dma = pltpu.SemaphoreType.DMA
-        vmem = pltpu.VMEM
+        vmem, small = pltpu.VMEM, pltpu.SMEM
         levels = bottom.reshape(TILE)
         base, tail = pl.pallas_call(
             functools.partial(kernel, parts),
-            out_shape=(jax.ShapeDtypeStruct(wide, f32), jax.ShapeDtypeStruct((3, *TILE), f32)),
-            in_specs=[hbm] * 6 + [smem] * 2,
-            out_specs=(hbm, hbm),
+            out_shape=(vmem(wide, f32), vmem((4 + GROUPS, *TILE), f32)),
+            in_specs=[hbm] * 9,
+            out_specs=(inner, inner),
             scratch_shapes=[
                 vmem(wide, f32), vmem(TILE, i32), vmem((6, ROWS * BLOCK), i32), vmem((6, ROWS * BLOCK), f32),
-                vmem(TILE, f32), vmem(TILE, f32), vmem(wide, f32), vmem((3, *TILE), f32),
+                vmem(TILE, f32), vmem(TILE, f32), small((1, 2, 4), i32), small((LEV,), f32), small((LEV,), f32),
                 vmem((4, 2, LEV, BLOCK), f32), vmem((4, 2, LEV, BLOCK), f32),
                 vmem((4, 2, BLOCK), f32), vmem((4, 2, BLOCK), f32), vmem(TILE, i32), vmem((4, *TILE), i32),
                 vmem((4, 2, *TILE), i32), vmem((4, 2, *TILE), i32), vmem((4, 2, *TILE), f32), vmem((4, 2, *TILE), f32),
@@ -430,19 +423,19 @@
                 vmem((ROUNDS, 4, 2, BLOCK), f32), vmem((ROUNDS, 2, 2, 2, BLOCK), f32), vmem((ROUNDS, 2, 1, 2, BLOCK), f32),
                 vmem((ROUNDS, 4, 2, BLOCK), f32), vmem((ROUNDS, 4, 2, BLOCK), f32),
                 vmem((6, *TILE), i32), vmem((6, *TILE), i32), vmem((6, *TILE), f32), vmem((6, *TILE), f32), vmem(TILE, f32),
-                dma((6,)), dma((2,)), dma((4, 2)), dma((4, 2)), dma((4, 2)), dma((4, 2)), dma((4, 2)),
+                dma((9,)), dma((4, 2)), dma((4, 2)), dma((4, 2)), dma((4, 2)), dma((4, 2)),
                 dma((ROUNDS, 4, 2)), dma((ROUNDS, 4, 2)), dma((ROUNDS, 4, 2)),
             ],
             compiler_params=pltpu.CompilerParams(collective_id=0, has_side_effects=True),
-        )(tracer, levels, near, weight, ssh.reshape(TILE), velocity.reshape(TILE), jnp.transpose(slots, (0, 2, 1)), thickness)
+        )(tracer, levels, near, weight, ssh.reshape(TILE), velocity.reshape(TILE), jnp.transpose(slots, (0, 2, 1)), thickness, profile)
         tile = jax.ShapeDtypeStruct(TILE, f32)
         out = pl.pallas_call(
             finish,
             out_shape=(jax.ShapeDtypeStruct(wide, f32), tile, tile),
-            in_specs=[hbm] * 3 + [smem],
+            in_specs=[inner] * 2,
             out_specs=(hbm, hbm, hbm),
-            scratch_shapes=[vmem(wide, f32), vmem((3, *TILE), f32), vmem(TILE, i32), dma((3,)), dma((3,))],
-        )(base, tail, levels, profile)
+            scratch_shapes=[vmem(wide, f32), dma((ROWS + 2,))],
+        )(*(pltpu.with_memory_space_constraint(x, pltpu.VMEM) for x in (base, tail)))
         return out[0], out[1].reshape(-1), out[2].reshape(-1)
 
     placed = (P(None, "dom"), P("dom"), P(None, "dom"), P(None, "dom"), P("dom"), P("dom"), P("dom", None, None), P(), P())

time: 29.5 us -> 27.1 us (0.919)
  Pallas kernels: 28.5 us -> 26.3 us
    pallas_call x1, Pallas kernels: 2.36 us -> 0.77 us  [shards(): pl.pallas_call(finish, out_shape=(jax.ShapeDtypeStruct(wide, f32), tile,...]
    pallas_call x1, Pallas kernels: 26.2 us -> 25.5 us  [shards(): pl.pallas_call(functools.partial(kernel, parts), out_shape=(vmem(wide, f3...]
where the time goes in v3:
time: 27.1 us; the launch traced here: 26.9 us
  Pallas kernels  26.3 us (97%)
  between operations  0.64 us (2%)
    pallas_call x1, Pallas kernels, shards(): pl.pallas_call(functools.partial(kernel, parts), out_shape=(vmem(wide, f3...  25.5 us
    pallas_call x1, Pallas kernels, shards(): pl.pallas_call(finish, out_shape=(jax.ShapeDtypeStruct(wide, f32), tile,...  0.77 us

profile of v3, /device:TPU:384, one launch (start us, length us, event | category | flops | bytes accessed | tf_op | source)
XLA Modules:
  0.0 26.9 jit_solution(11469361340354528709)
XLA Ops:
  0.6 25.5 %shard_map.112 = (f32[40,1024]{1,0:T(8,128)S(1)}, f32[9,8,128]{2,1,0:T(8,128)S(1)}) custom-call(f32[40,1024]{1,0:T(8,128)} %tracer_hbm.1, s32[8,128]{1,0:T(8,128)} %bitcast.6, s32[6,1024]{1,0:T(8,128)} %near_hbm.1, f32[6,1024]{1,0:T(8,128)} %weight_hbm.1, f32[8,128]{1,0:T(8,128)} %bitcast.7, f32[8,128]{1,0:T(8,128)} %bitcast.8, s32[1,2,4]{2,1,0:T(2,128)} %bitcast.9, ...), custom_call_target="tpu_custom_call" | custom-call | tf_op jit(solution)/shard_map/pallas_call | solution.py:411
  26.2 0.8 %shard_map.113 = (f32[40,1024]{1,0:T(8,128)}, f32[8,128]{1,0:T(8,128)}, f32[8,128]{1,0:T(8,128)}) custom-call(f32[40,1024]{1,0:T(8,128)S(1)} %get-tuple-element.8.base_v, f32[9,8,128]{2,1,0:T(8,128)S(1)} %get-tuple-element.9.tail_v), custom_call_target="tpu_custom_call" | custom-call | tf_op jit(solution)/shard_map/pallas_call | solution.py:432

commit v4 on v3

--- a/solution.py
+++ b/solution.py
@@ -45,7 +45,7 @@
     base_v, tail_v,
     tracer_v, bottom_v, near_v, weight_v, ssh_v, velocity_v, slots, thickness, profile,
     send_tracer, halo_tracer, send_level, halo_level, send_chosen, halo_chosen,
-    send_near, halo_near, send_weight, halo_weight,
+    send_near, halo_near, send_weight, halo_weight, outer_row, outer_lane, outer_weight,
     send_height, halo_height, send_picked, halo_three, halo_four, send_push, halo_push,
     near_row, near_lane, weight_s, near_level, forcing_v,
     copy_sem, tracer_sem, level_sem, chosen_sem, near_sem, weight_sem, height_sem, far_sem, push_sem,
@@ -77,6 +77,7 @@
     velocity_copy = start(velocity_hbm, velocity_v, 5)
 
     row_id = lax.broadcasted_iota(jnp.int32, TILE, 0)
+    partner_id = row_id >> 1
     level_f = row_id.astype(jnp.float32)
     zero = jnp.zeros(TILE, jnp.float32)
 
@@ -84,8 +85,8 @@
         @pl.when(jnp.logical_not(inside(me - OFFSETS[number])))
         def _(number=number):
             halo_chosen[number] = jnp.full(TILE, -1, jnp.int32)
-            halo_near[number] = jnp.full((2, *TILE), LAND, jnp.int32)
-            halo_weight[number] = jnp.zeros((2, *TILE), jnp.float32)
+            halo_near[number] = jnp.full((6, 2, BLOCK), LAND, jnp.int32)
+            halo_weight[number] = jnp.zeros((6, 2, BLOCK), jnp.float32)
             halo_level[number] = jnp.zeros((2, BLOCK), jnp.float32)
             halo_tracer[number] = jnp.zeros((2, LEV, BLOCK), jnp.float32)
             for turn in range(ROUNDS):
@@ -208,18 +209,6 @@
 
     near_copy.wait()
     weight_copy.wait()
-    for place in range(ROWS):
-        which = spread(chosen[place:place + 1])
-        n, slot = place // 2, place % 2
-        index = jnp.full((6, BLOCK), LAND, jnp.int32)
-        amount = jnp.zeros((6, BLOCK), jnp.float32)
-        for block in range(ROWS):
-            index = jnp.where(which[:6] == block, near_v[:, cols(block)], index)
-            amount = jnp.where(which[:6] == block, weight_v[:, cols(block)], amount)
-        send_near[n, slot] = jnp.full(TILE, LAND, jnp.int32)
-        send_weight[n, slot] = zero
-        send_near[n, slot, 0:6] = index
-        send_weight[n, slot, 0:6] = amount
     total_weight = zero
     for column in range(6):
         for block in range(ROWS):
@@ -227,9 +216,15 @@
             weight_s[column, block:block + 1] = weight_v[column:column + 1, cols(block)]
     for column in range(6):
         index = near_row[column]
+        weight = weight_s[column]
+        total_weight = total_weight + weight
+        sent_index = along(index, jnp.maximum(chosen, 0), 0)
+        sent_weight = pick(weight, chosen)
+        for number in range(4):
+            send_near[number, column] = sent_index[2 * number:2 * number + 2]
+            send_weight[number, column] = sent_weight[2 * number:2 * number + 2]
         near_lane[column] = index & (BLOCK - 1)
         near_row[column] = index >> 7
-        total_weight = total_weight + weight_s[column]
     for place in range(ROWS):
         which = spread(chosen[place:place + 1])
         for group in range(GROUPS):
@@ -239,8 +234,11 @@
             send_tracer[place // 2, place % 2, pl.ds(group * 8, 8), :] = piece
 
     pl.semaphore_wait(barrier, sum(inside(me + offset).astype(jnp.int32) for offset in OFFSETS + FAR))
+    begin([functools.partial(height_link, 0)])
+    begin([chosen_link])
     begin([functools.partial(far_link, 0)], FAR)
-    begin([functools.partial(height_link, 0), chosen_link, near_link, weight_link, functools.partial(push_link, 0)])
+    begin([near_link, weight_link])
+    begin([functools.partial(push_link, 0)])
     begin([level_link, tracer_link])
 
     def gather(rows, first_row, columns, sums):
@@ -302,49 +300,76 @@
         if turn >= 1:
             lax.fori_loop(4 * (turn - 1), 4 * turn, tracer_block, 0)
         sums = gather(height, 0, own_columns(), [zero] * 6)
-        arrive([functools.partial(height_link, turn)] + ([chosen_link] if turn == 0 else []))
+        if turn == ROUNDS - 1:
+            leave([chosen_link, near_link, weight_link, level_link, tracer_link])
+            for earlier in range(ROUNDS):
+                leave([functools.partial(far_link, earlier)], FAR)
+                leave([functools.partial(height_link, earlier), functools.partial(push_link, earlier)])
+        arrive([functools.partial(height_link, turn), functools.partial(push_link, turn)] + ([chosen_link, near_link, weight_link] if turn == 0 else []))
+        if turn == 0:
+            for column in range(6):
+                index = jnp.concatenate([halo_near[n, column] for n in range(4)], axis=0)
+                outer_lane[column] = index & (BLOCK - 1)
+                outer_row[column] = index >> 7
+                outer_weight[column] = jnp.concatenate([halo_weight[n, column] for n in range(4)], axis=0)
         fields = [halo_height[turn, n] for n in range(4)]
         choices = [halo_chosen[n] for n in range(4)]
         picks = [pick(fields[n], choices[n]) for n in range(4)]
         halo = jnp.concatenate([picks[n][2 * n:2 * n + 2] for n in range(4)], axis=0)
         alive = jnp.concatenate([choices[n][2 * n:2 * n + 2] for n in range(4)], axis=0)
         sums = gather(halo, ROWS, own_columns(), sums)
-        arrive([functools.partial(push_link, turn)] + ([near_link, weight_link] if turn == 0 else []))
+
+        def mixed(rows):
+            tile = zero
+            for h in range(4):
+                if rows[h] is not None:
+                    tile = jnp.where(partner_id == h, spread(rows[h]), tile)
+            return tile
+
+        def outer_gather(tiles):
+            found = [zero] * 6
+            for column in range(6):
+                row = outer_row[column]
+                lane = outer_lane[column]
+                for r, tile in tiles:
+                    found[column] = jnp.where(row == r, along(tile, lane, 1), found[column])
+            total = zero
+            for column in range(6):
+                total = total + outer_weight[column] * found[column]
+            return total
+
+        tiles = [(r, mixed([fields[h][r:r + 1] for h in range(4)])) for r in range(ROWS)]
+        for g in range(4):
+            gaps = [OFFSETS[h] + OFFSETS[g] for h in range(4)]
+            for slot in range(2):
+                at = 2 * g + slot
+                rows = [picked[at:at + 1] if gap == 0 else picks[OFFSETS.index(gap)][at:at + 1] if gap in OFFSETS else None for gap in gaps]
+                tiles.append((ROWS + at, mixed(rows)))
         outer = jnp.concatenate([halo_push[turn, n] for n in range(4)], axis=0)
-
-        def partner_columns(h):
-            indices = [halo_near[h, slot] for slot in range(2)]
-            return [(index >> 7, index & (BLOCK - 1)) for index in indices]
-
-        found = []
-        for h in range(4):
-            got = gather(fields[h], 0, partner_columns(h), [zero] * 2)
-            for g in range(4):
-                gap = OFFSETS[h] + OFFSETS[g]
-                if gap == 0 or gap in OFFSETS:
-                    rows = picked if gap == 0 else picks[OFFSETS.index(gap)]
-                    got = gather(rows[2 * g:2 * g + 2], ROWS + 2 * g, partner_columns(h), got)
-            found.append(got)
+        weight = zero
+        for column in range(6):
+            weight = weight + outer_weight[column]
+        outer = outer + barotropic_step * (outer_gather(tiles) - weight * halo)
         speed, height = own_update(sums, height, push)
         push = pushed_by(speed)
         summed = summed + speed
         sums = gather(height, 0, own_columns(), [zero] * 6)
 
         arrive([functools.partial(far_link, turn)], FAR)
-        laplaces = []
-        for h in range(4):
-            for g in range(4):
-                gap = OFFSETS[h] + OFFSETS[g]
-                if gap in FAR:
-                    f = FAR.index(gap)
-                    at = PLACE[g] - FAR_ROWS[f][0]
-                    rows = halo_three[turn, f, at] if f < 2 else halo_four[turn, f - 2, at]
-                    found[h] = gather(rows, ROWS + 2 * g, partner_columns(h), found[h])
+        tiles = []
+        for g in range(4):
+            gaps = [OFFSETS[h] + OFFSETS[g] for h in range(4)]
             for slot in range(2):
-                place = 2 * h + slot
-                difference = halo_weight[h, slot] * (found[h][slot] - spread(halo[place:place + 1]))
-                laplaces.append(jnp.sum(difference, axis=0, keepdims=True))
-        outer = outer + barotropic_step * jnp.concatenate(laplaces, axis=0)
+                rows = []
+                for gap in gaps:
+                    if gap in FAR:
+                        f = FAR.index(gap)
+                        at = PLACE[g] - FAR_ROWS[f][0]
+                        rows.append((halo_three[turn, f, at] if f < 2 else halo_four[turn, f - 2, at])[slot:slot + 1])
+                    else:
+                        rows.append(None)
+                tiles.append((ROWS + 2 * g + slot, mixed(rows)))
+        outer = outer + barotropic_step * outer_gather(tiles)
         halo = jnp.where(alive >= 0, halo + barotropic_step * outer, 0.0)
         sums = gather(halo, ROWS, own_columns(), sums)
         speed, height = own_update(sums, height, push)
@@ -352,8 +377,9 @@
         summed = summed + speed
         if turn < ROUNDS - 1:
             picked = put_round(turn + 1, height, push)
+            begin([functools.partial(height_link, turn + 1)])
             begin([functools.partial(far_link, turn + 1)], FAR)
-            begin([functools.partial(height_link, turn + 1), functools.partial(push_link, turn + 1)])
+            begin([functools.partial(push_link, turn + 1)])
         if turn == 0:
             arrive([level_link])
             depths = gather(levels, 0, own_columns(), [zero] * 6)
@@ -365,10 +391,6 @@
     tail_v[0] = height
     tail_v[1] = speed
     tail_v[2] = summed * (1.0 / SUBSTEPS)
-    for turn in range(ROUNDS):
-        leave([functools.partial(far_link, turn)], FAR)
-        leave([functools.partial(height_link, turn), functools.partial(push_link, turn)])
-    leave([chosen_link, near_link, weight_link, level_link, tracer_link])
 
 
 def finish(base_v, tail_v, tracer_out, ssh_out, velocity_out, result_v, out_sem):
@@ -418,7 +440,8 @@
                 vmem(TILE, f32), vmem(TILE, f32), small((1, 2, 4), i32), small((LEV,), f32), small((LEV,), f32),
                 vmem((4, 2, LEV, BLOCK), f32), vmem((4, 2, LEV, BLOCK), f32),
                 vmem((4, 2, BLOCK), f32), vmem((4, 2, BLOCK), f32), vmem(TILE, i32), vmem((4, *TILE), i32),
-                vmem((4, 2, *TILE), i32), vmem((4, 2, *TILE), i32), vmem((4, 2, *TILE), f32), vmem((4, 2, *TILE), f32),
+                vmem((4, 6, 2, BLOCK), i32), vmem((4, 6, 2, BLOCK), i32), vmem((4, 6, 2, BLOCK), f32), vmem((4, 6, 2, BLOCK), f32),
+                vmem((6, *TILE), i32), vmem((6, *TILE), i32), vmem((6, *TILE), f32),
                 vmem((ROUNDS, *TILE), f32), vmem((ROUNDS, 4, *TILE), f32),
                 vmem((ROUNDS, 4, 2, BLOCK), f32), vmem((ROUNDS, 2, 2, 2, BLOCK), f32), vmem((ROUNDS, 2, 1, 2, BLOCK), f32),
                 vmem((ROUNDS, 4, 2, BLOCK), f32), vmem((ROUNDS, 4, 2, BLOCK), f32),

time: 27.1 us -> 26.6 us (0.982)
  Pallas kernels: 26.3 us -> 25.9 us
    pallas_call x1, Pallas kernels: 25.5 us -> 25.1 us  [shards(): pl.pallas_call(functools.partial(kernel, parts), out_shape=(vmem(wide, f3...]
where the time goes in v4:
time: 26.6 us; the launch traced here: 26.5 us
  Pallas kernels  25.9 us (97%)
  between operations  0.64 us (2%)
    pallas_call x1, Pallas kernels, shards(): pl.pallas_call(functools.partial(kernel, parts), out_shape=(vmem(wide, f3...  25.1 us
    pallas_call x1, Pallas kernels, shards(): pl.pallas_call(finish, out_shape=(jax.ShapeDtypeStruct(wide, f32), tile,...  0.77 us

profile of v4, /device:TPU:384, one launch (start us, length us, event | category | flops | bytes accessed | tf_op | source)
XLA Modules:
  0.0 26.5 jit_solution(5416151681205329174)
XLA Ops:
  0.6 25.1 %shard_map.112 = (f32[40,1024]{1,0:T(8,128)S(1)}, f32[9,8,128]{2,1,0:T(8,128)S(1)}) custom-call(f32[40,1024]{1,0:T(8,128)} %tracer_hbm.1, s32[8,128]{1,0:T(8,128)} %bitcast.6, s32[6,1024]{1,0:T(8,128)} %near_hbm.1, f32[6,1024]{1,0:T(8,128)} %weight_hbm.1, f32[8,128]{1,0:T(8,128)} %bitcast.7, f32[8,128]{1,0:T(8,128)} %bitcast.8, s32[1,2,4]{2,1,0:T(2,128)} %bitcast.9, ...), custom_call_target="tpu_custom_call" | custom-call | tf_op jit(solution)/shard_map/pallas_call | solution.py:433
  25.7 0.8 %shard_map.113 = (f32[40,1024]{1,0:T(8,128)}, f32[8,128]{1,0:T(8,128)}, f32[8,128]{1,0:T(8,128)}) custom-call(f32[40,1024]{1,0:T(8,128)S(1)} %get-tuple-element.8.base_v, f32[9,8,128]{2,1,0:T(8,128)S(1)} %get-tuple-element.9.tail_v), custom_call_target="tpu_custom_call" | custom-call | tf_op jit(solution)/shard_map/pallas_call | solution.py:455

commit v5 on v4

--- a/solution.py
+++ b/solution.py
@@ -44,11 +44,11 @@
     parts, tracer_hbm, bottom_hbm, near_hbm, weight_hbm, ssh_hbm, velocity_hbm, slots_hbm, thickness_hbm, profile_hbm,
     base_v, tail_v,
     tracer_v, bottom_v, near_v, weight_v, ssh_v, velocity_v, slots, thickness, profile,
-    send_tracer, halo_tracer, send_level, halo_level, send_chosen, halo_chosen,
-    send_near, halo_near, send_weight, halo_weight, outer_row, outer_lane, outer_weight,
-    send_height, halo_height, send_picked, halo_three, halo_four, send_push, halo_push,
+    send_tracer, halo_tracer,
+    send_whole, halo_whole, send_real, halo_real, outer_row, outer_lane, outer_weight,
+    send_height, halo_height, send_picked, halo_three, halo_four,
     near_row, near_lane, weight_s, near_level, forcing_v,
-    copy_sem, tracer_sem, level_sem, chosen_sem, near_sem, weight_sem, height_sem, far_sem, push_sem,
+    copy_sem, tracer_sem, whole_sem, real_sem, height_sem, far_sem,
 ):
     me = lax.axis_index("dom")
 
@@ -84,14 +84,12 @@
     for number in range(4):
         @pl.when(jnp.logical_not(inside(me - OFFSETS[number])))
         def _(number=number):
-            halo_chosen[number] = jnp.full(TILE, -1, jnp.int32)
-            halo_near[number] = jnp.full((6, 2, BLOCK), LAND, jnp.int32)
-            halo_weight[number] = jnp.zeros((6, 2, BLOCK), jnp.float32)
-            halo_level[number] = jnp.zeros((2, BLOCK), jnp.float32)
+            halo_whole[number, 0:ROWS] = jnp.full(TILE, -1, jnp.int32)
+            halo_whole[number, ROWS:ROWS + 12] = jnp.full((12, BLOCK), LAND, jnp.int32)
+            halo_real[number] = jnp.zeros((14, BLOCK), jnp.float32)
             halo_tracer[number] = jnp.zeros((2, LEV, BLOCK), jnp.float32)
             for turn in range(ROUNDS):
-                halo_height[turn, number] = zero
-                halo_push[turn, number] = jnp.zeros((2, BLOCK), jnp.float32)
+                halo_height[turn, number] = jnp.zeros((ROWS + 2, BLOCK), jnp.float32)
         @pl.when(jnp.logical_not(inside(me - FAR[number])))
         def _(number=number):
             for turn in range(ROUNDS):
@@ -108,23 +106,14 @@
     def tracer_link(n):
         return remote(send_tracer.at[n], halo_tracer.at[n], tracer_sem.at[n], OFFSETS[n])
 
-    def level_link(n):
-        return remote(send_level.at[n], halo_level.at[n], level_sem.at[n], OFFSETS[n])
-
-    def chosen_link(n):
-        return remote(send_chosen, halo_chosen.at[n], chosen_sem.at[n], OFFSETS[n])
-
-    def near_link(n):
-        return remote(send_near.at[n], halo_near.at[n], near_sem.at[n], OFFSETS[n])
-
-    def weight_link(n):
-        return remote(send_weight.at[n], halo_weight.at[n], weight_sem.at[n], OFFSETS[n])
+    def whole_link(n):
+        return remote(send_whole.at[n], halo_whole.at[n], whole_sem.at[n], OFFSETS[n])
+
+    def real_link(n):
+        return remote(send_real.at[n], halo_real.at[n], real_sem.at[n], OFFSETS[n])
 
     def height_link(turn, n):
-        return remote(send_height.at[turn], halo_height.at[turn, n], height_sem.at[turn, n], OFFSETS[n])
-
-    def push_link(turn, n):
-        return remote(send_push.at[turn, n], halo_push.at[turn, n], push_sem.at[turn, n], OFFSETS[n])
+        return remote(send_height.at[turn, n], halo_height.at[turn, n], height_sem.at[turn, n], OFFSETS[n])
 
     def far_link(turn, n):
         low, high = FAR_ROWS[n]
@@ -157,7 +146,8 @@
     for number in range(4):
         for slot in range(2):
             chosen = jnp.where(row_id == 2 * number + slot, slots[0, slot, number], chosen)
-    send_chosen[...] = chosen
+    for number in range(4):
+        send_whole[number, 0:ROWS] = chosen
 
     def pick(values, choice):
         return jnp.where(choice >= 0, along(values, jnp.maximum(choice, 0), 0), 0.0)
@@ -165,17 +155,17 @@
     def put_round(turn, height, push):
         picked = pick(height, chosen)
         pushed = pick(push, chosen)
-        send_height[turn] = height
         for number in range(4):
             send_picked[turn, PLACE[number]] = picked[2 * number:2 * number + 2]
-            send_push[turn, number] = pushed[2 * number:2 * number + 2]
+            send_height[turn, number, 0:ROWS] = height
+            send_height[turn, number, ROWS:ROWS + 2] = pushed[2 * number:2 * number + 2]
         return picked
 
     bottom_copy.wait()
     levels = bottom_v[...].astype(jnp.float32)
     sent_levels = pick(levels, chosen)
     for number in range(4):
-        send_level[number] = sent_levels[2 * number:2 * number + 2]
+        send_real[number, 12:14] = sent_levels[2 * number:2 * number + 2]
     thickness_copy.wait()
     profile_copy.wait()
     thick = []
@@ -221,8 +211,8 @@
         sent_index = along(index, jnp.maximum(chosen, 0), 0)
         sent_weight = pick(weight, chosen)
         for number in range(4):
-            send_near[number, column] = sent_index[2 * number:2 * number + 2]
-            send_weight[number, column] = sent_weight[2 * number:2 * number + 2]
+            send_whole[number, ROWS + 2 * column:ROWS + 2 * column + 2] = sent_index[2 * number:2 * number + 2]
+            send_real[number, 2 * column:2 * column + 2] = sent_weight[2 * number:2 * number + 2]
         near_lane[column] = index & (BLOCK - 1)
         near_row[column] = index >> 7
     for place in range(ROWS):
@@ -235,11 +225,9 @@
 
     pl.semaphore_wait(barrier, sum(inside(me + offset).astype(jnp.int32) for offset in OFFSETS + FAR))
     begin([functools.partial(height_link, 0)])
-    begin([chosen_link])
     begin([functools.partial(far_link, 0)], FAR)
-    begin([near_link, weight_link])
-    begin([functools.partial(push_link, 0)])
-    begin([level_link, tracer_link])
+    begin([whole_link, real_link])
+    begin([tracer_link])
 
     def gather(rows, first_row, columns, sums):
         sums = list(sums)
@@ -301,19 +289,19 @@
             lax.fori_loop(4 * (turn - 1), 4 * turn, tracer_block, 0)
         sums = gather(height, 0, own_columns(), [zero] * 6)
         if turn == ROUNDS - 1:
-            leave([chosen_link, near_link, weight_link, level_link, tracer_link])
+            leave([whole_link, real_link, tracer_link])
             for earlier in range(ROUNDS):
                 leave([functools.partial(far_link, earlier)], FAR)
-                leave([functools.partial(height_link, earlier), functools.partial(push_link, earlier)])
-        arrive([functools.partial(height_link, turn), functools.partial(push_link, turn)] + ([chosen_link, near_link, weight_link] if turn == 0 else []))
+                leave([functools.partial(height_link, earlier)])
+        arrive([functools.partial(height_link, turn)] + ([whole_link, real_link] if turn == 0 else []))
         if turn == 0:
             for column in range(6):
-                index = jnp.concatenate([halo_near[n, column] for n in range(4)], axis=0)
+                index = jnp.concatenate([halo_whole[n, ROWS + 2 * column:ROWS + 2 * column + 2] for n in range(4)], axis=0)
                 outer_lane[column] = index & (BLOCK - 1)
                 outer_row[column] = index >> 7
-                outer_weight[column] = jnp.concatenate([halo_weight[n, column] for n in range(4)], axis=0)
-        fields = [halo_height[turn, n] for n in range(4)]
-        choices = [halo_chosen[n] for n in range(4)]
+                outer_weight[column] = jnp.concatenate([halo_real[n, 2 * column:2 * column + 2] for n in range(4)], axis=0)
+        fields = [halo_height[turn, n, 0:ROWS] for n in range(4)]
+        choices = [halo_whole[n, 0:ROWS] for n in range(4)]
         picks = [pick(fields[n], choices[n]) for n in range(4)]
         halo = jnp.concatenate([picks[n][2 * n:2 * n + 2] for n in range(4)], axis=0)
         alive = jnp.concatenate([choices[n][2 * n:2 * n + 2] for n in range(4)], axis=0)
@@ -345,7 +333,7 @@
                 at = 2 * g + slot
                 rows = [picked[at:at + 1] if gap == 0 else picks[OFFSETS.index(gap)][at:at + 1] if gap in OFFSETS else None for gap in gaps]
                 tiles.append((ROWS + at, mixed(rows)))
-        outer = jnp.concatenate([halo_push[turn, n] for n in range(4)], axis=0)
+        outer = jnp.concatenate([halo_height[turn, n, ROWS:ROWS + 2] for n in range(4)], axis=0)
         weight = zero
         for column in range(6):
             weight = weight + outer_weight[column]
@@ -379,11 +367,9 @@
             picked = put_round(turn + 1, height, push)
             begin([functools.partial(height_link, turn + 1)])
             begin([functools.partial(far_link, turn + 1)], FAR)
-            begin([functools.partial(push_link, turn + 1)])
         if turn == 0:
-            arrive([level_link])
             depths = gather(levels, 0, own_columns(), [zero] * 6)
-            around = jnp.concatenate([halo_level[n] for n in range(4)], axis=0)
+            around = jnp.concatenate([halo_real[n, 12:14] for n in range(4)], axis=0)
             depths = gather(around, ROWS, own_columns(), depths)
             for column in range(6):
                 near_level[column] = depths[column]
@@ -439,15 +425,13 @@
                 vmem(wide, f32), vmem(TILE, i32), vmem((6, ROWS * BLOCK), i32), vmem((6, ROWS * BLOCK), f32),
                 vmem(TILE, f32), vmem(TILE, f32), small((1, 2, 4), i32), small((LEV,), f32), small((LEV,), f32),
                 vmem((4, 2, LEV, BLOCK), f32), vmem((4, 2, LEV, BLOCK), f32),
-                vmem((4, 2, BLOCK), f32), vmem((4, 2, BLOCK), f32), vmem(TILE, i32), vmem((4, *TILE), i32),
-                vmem((4, 6, 2, BLOCK), i32), vmem((4, 6, 2, BLOCK), i32), vmem((4, 6, 2, BLOCK), f32), vmem((4, 6, 2, BLOCK), f32),
+                                vmem((4, ROWS + 12, BLOCK), i32), vmem((4, ROWS + 12, BLOCK), i32), vmem((4, 14, BLOCK), f32), vmem((4, 14, BLOCK), f32),
                 vmem((6, *TILE), i32), vmem((6, *TILE), i32), vmem((6, *TILE), f32),
-                vmem((ROUNDS, *TILE), f32), vmem((ROUNDS, 4, *TILE), f32),
+                vmem((ROUNDS, 4, ROWS + 2, BLOCK), f32), vmem((ROUNDS, 4, ROWS + 2, BLOCK), f32),
                 vmem((ROUNDS, 4, 2, BLOCK), f32), vmem((ROUNDS, 2, 2, 2, BLOCK), f32), vmem((ROUNDS, 2, 1, 2, BLOCK), f32),
-                vmem((ROUNDS, 4, 2, BLOCK), f32), vmem((ROUNDS, 4, 2, BLOCK), f32),
                 vmem((6, *TILE), i32), vmem((6, *TILE), i32), vmem((6, *TILE), f32), vmem((6, *TILE), f32), vmem(TILE, f32),
-                dma((9,)), dma((4, 2)), dma((4, 2)), dma((4, 2)), dma((4, 2)), dma((4, 2)),
-                dma((ROUNDS, 4, 2)), dma((ROUNDS, 4, 2)), dma((ROUNDS, 4, 2)),
+                dma((9,)), dma((4, 2)), dma((4, 2)), dma((4, 2)),
+                dma((ROUNDS, 4, 2)), dma((ROUNDS, 4, 2)),
             ],
             compiler_params=pltpu.CompilerParams(collective_id=0, has_side_effects=True),
         )(tracer, levels, near, weight, ssh.reshape(TILE), velocity.reshape(TILE), jnp.transpose(slots, (0, 2, 1)), thickness, profile)

time: 26.6 us -> 26.1 us (0.981)
  the two profiles are of different devices: /device:TPU:384 before, /device:TPU:256 now
where the time goes in v5:
time: 26.1 us; the launch traced here: 26 us
  Pallas kernels  25.4 us (97%)
  between operations  0.64 us (2%)
    pallas_call x1, Pallas kernels, shards(): pl.pallas_call(functools.partial(kernel, parts), out_shape=(vmem(wide, f3...  24.6 us
    pallas_call x1, Pallas kernels, shards(): pl.pallas_call(finish, out_shape=(jax.ShapeDtypeStruct(wide, f32), tile,...  0.77 us

profile of v5, /device:TPU:256, one launch (start us, length us, event | category | flops | bytes accessed | tf_op | source)
XLA Modules:
  0.0 26.0 jit_solution(5921573099503856772)
XLA Ops:
  0.6 24.6 %shard_map.112 = (f32[40,1024]{1,0:T(8,128)S(1)}, f32[9,8,128]{2,1,0:T(8,128)S(1)}) custom-call(f32[40,1024]{1,0:T(8,128)} %tracer_hbm.1, s32[8,128]{1,0:T(8,128)} %bitcast.6, s32[6,1024]{1,0:T(8,128)} %near_hbm.1, f32[6,1024]{1,0:T(8,128)} %weight_hbm.1, f32[8,128]{1,0:T(8,128)} %bitcast.7, f32[8,128]{1,0:T(8,128)} %bitcast.8, s32[1,2,4]{2,1,0:T(2,128)} %bitcast.9, ...), custom_call_target="tpu_custom_call" | custom-call | tf_op jit(solution)/shard_map/pallas_call | solution.py:419
  25.2 0.8 %shard_map.113 = (f32[40,1024]{1,0:T(8,128)}, f32[8,128]{1,0:T(8,128)}, f32[8,128]{1,0:T(8,128)}) custom-call(f32[40,1024]{1,0:T(8,128)S(1)} %get-tuple-element.8.base_v, f32[9,8,128]{2,1,0:T(8,128)S(1)} %get-tuple-element.9.tail_v), custom_call_target="tpu_custom_call" | custom-call | tf_op jit(solution)/shard_map/pallas_call | solution.py:439

commit v6 on v5

--- a/solution.py
+++ b/solution.py
@@ -327,12 +327,17 @@
             return total
 
         tiles = [(r, mixed([fields[h][r:r + 1] for h in range(4)])) for r in range(ROWS)]
-        for g in range(4):
-            gaps = [OFFSETS[h] + OFFSETS[g] for h in range(4)]
-            for slot in range(2):
-                at = 2 * g + slot
-                rows = [picked[at:at + 1] if gap == 0 else picks[OFFSETS.index(gap)][at:at + 1] if gap in OFFSETS else None for gap in gaps]
-                tiles.append((ROWS + at, mixed(rows)))
+        def close_row(h, g, slot):
+            gap, at = OFFSETS[h] + OFFSETS[g], 2 * g + slot
+            if gap == 0:
+                return picked[at:at + 1]
+            return picks[OFFSETS.index(gap)][at:at + 1] if gap in OFFSETS else None
+
+        apart = 2 * (partner_id & 1)
+        for slot in range(2):
+            tiles.append((ROWS + slot, mixed([close_row(h, 0, slot) for h in range(4)])))
+            tiles.append((ROWS + 2 + slot, mixed([close_row(h, 1, slot) for h in range(4)])))
+            tiles.append((ROWS + 6 + slot - apart, mixed([close_row(h, 3 - h % 2, slot) for h in range(4)])))
         outer = jnp.concatenate([halo_height[turn, n, ROWS:ROWS + 2] for n in range(4)], axis=0)
         weight = zero
         for column in range(6):
@@ -345,18 +350,19 @@
 
         arrive([functools.partial(far_link, turn)], FAR)
         tiles = []
-        for g in range(4):
-            gaps = [OFFSETS[h] + OFFSETS[g] for h in range(4)]
+        for first in (0, 2):
             for slot in range(2):
                 rows = []
-                for gap in gaps:
+                for h in range(4):
+                    g = first + h % 2
+                    gap = OFFSETS[h] + OFFSETS[g]
                     if gap in FAR:
                         f = FAR.index(gap)
                         at = PLACE[g] - FAR_ROWS[f][0]
                         rows.append((halo_three[turn, f, at] if f < 2 else halo_four[turn, f - 2, at])[slot:slot + 1])
                     else:
                         rows.append(None)
-                tiles.append((ROWS + 2 * g + slot, mixed(rows)))
+                tiles.append((ROWS + 2 * first + slot + apart, mixed(rows)))
         outer = outer + barotropic_step * outer_gather(tiles)
         halo = jnp.where(alive >= 0, halo + barotropic_step * outer, 0.0)
         sums = gather(halo, ROWS, own_columns(), sums)

time: 26.1 us -> 26 us (level)
  the two profiles are of different devices: /device:TPU:256 before, /device:TPU:384 now
where the time goes in v6:
time: 26 us; the launch traced here: 25.9 us
  Pallas kernels  25.3 us (97%)
  between operations  0.64 us (2%)
    pallas_call x1, Pallas kernels, shards(): pl.pallas_call(functools.partial(kernel, parts), out_shape=(vmem(wide, f3...  24.5 us
    pallas_call x1, Pallas kernels, shards(): pl.pallas_call(finish, out_shape=(jax.ShapeDtypeStruct(wide, f32), tile,...  0.77 us

profile of v6, /device:TPU:384, one launch (start us, length us, event | category | flops | bytes accessed | tf_op | source)
XLA Modules:
  0.0 25.9 jit_solution(8013281880920469905)
XLA Ops:
  0.6 24.5 %shard_map.112 = (f32[40,1024]{1,0:T(8,128)S(1)}, f32[9,8,128]{2,1,0:T(8,128)S(1)}) custom-call(f32[40,1024]{1,0:T(8,128)} %tracer_hbm.1, s32[8,128]{1,0:T(8,128)} %bitcast.6, s32[6,1024]{1,0:T(8,128)} %near_hbm.1, f32[6,1024]{1,0:T(8,128)} %weight_hbm.1, f32[8,128]{1,0:T(8,128)} %bitcast.7, f32[8,128]{1,0:T(8,128)} %bitcast.8, s32[1,2,4]{2,1,0:T(2,128)} %bitcast.9, ...), custom_call_target="tpu_custom_call" | custom-call | tf_op jit(solution)/shard_map/pallas_call | solution.py:425
  25.1 0.8 %shard_map.113 = (f32[40,1024]{1,0:T(8,128)}, f32[8,128]{1,0:T(8,128)}, f32[8,128]{1,0:T(8,128)}) custom-call(f32[40,1024]{1,0:T(8,128)S(1)} %get-tuple-element.8.base_v, f32[9,8,128]{2,1,0:T(8,128)S(1)} %get-tuple-element.9.tail_v), custom_call_target="tpu_custom_call" | custom-call | tf_op jit(solution)/shard_map/pallas_call | solution.py:445
